TPU v7x, 32 devices: a whole 2x2x4 slice. The times are simulated.
32 devices in a mesh: ea: 4 (over y, x), row: 4 (over z), col: 2 (over core).
Axes of the slice: x: 2, y: 2, z: 4, core: 2. Of those that a mesh axis runs over, the one named last changes fastest.
Arguments:
- weights: float32 [4, 256, 2048], P('ea', 'row', 'col'), parts along dimension 0, may hold values from -6 to 6
- codebook: float32 [4, 16, 2, 256], P('ea', 'col'), parts along dimension 0, may hold values from -4 to 4
- assign: int32 [4, 256, 1024], P('ea', 'row', 'col'), parts along dimension 0, may hold values from 0 to 255
- chol_upper: float32 [4, 2048, 2048], P('ea', 'row', 'col'), parts along dimension 0, may hold values from 0 to 1.4, as said below
- inv_blocks: float32 [4, 16, 128, 128], P('ea', 'col'), parts along dimension 0, may hold values from -1 to 1.5, as said below
Outputs:
- errors: float32 [4, 256, 2048], P('ea', 'row', 'col'), parts along dimension 0
- row_loss: float32 [4, 256], P('ea', 'row'), parts along dimension 0
- codeword_mass: float32 [4, 16, 256], P('ea', 'col'), parts along dimension 0
There are 4 independent parts, one for each index of `ea`. A program takes and returns all parts, laid end to end along the dimension named above; each array names one. Nothing has to cross between parts.
Inputs may be any that keep to these rules, and one draw needn't show every extreme that they name: `chol_upper`: upper triangular with a positive diagonal. inv_blocks[x, b] is the inverse of the diagonal block of chol_upper[x] on rows and columns [b * 128, (b + 1) * 128).
All inputs are finite; a program needn't handle non-finite values.
Results may differ from a plain program's by a relative error of at most 0.0001.
Values sent between devices are 32-bit elements; how exact they have to be, the bound alone decides.
No kernel may reach another device: no remote copies, remote signals or barrier semaphores. Data moves between devices by JAX's collectives and lax.ppermute only.
A program may use at most 64 MiB of HBM per device.

v0:
```python
import jax
import jax.numpy as jnp
from jax import lax
from jax.sharding import PartitionSpec as P


def from_root(value, axis, source):
    kept = jnp.where(lax.axis_index(axis) == source, value, 0).astype(value.dtype)
    return lax.psum(kept, axis)


def flat_labels(assign, half_block, code_count):
    pair_count = assign.shape[2]
    offsets = jnp.arange(pair_count, dtype=jnp.int32) // half_block * code_count
    return assign + offsets[None, None, :]


def lookup_local(codebook, labels):
    experts, row_count, pair_count = labels.shape
    code_table = jnp.transpose(codebook, (0, 2, 1, 3)).reshape(experts, 2, -1)

    def select(rows_table, indices):
        return jnp.stack(
            [jnp.take(rows_table[0], indices), jnp.take(rows_table[1], indices)], axis=-1
        )

    picked = jax.vmap(select)(code_table, labels)
    return picked.reshape(experts, row_count, 2 * pair_count)


def mass_by_code(errors, labels, local_blocks, code_count):
    experts, row_count, width = errors.shape
    squared = errors * errors
    paired = squared.reshape(experts, row_count, width // 2, 2).sum(axis=3)

    def summed(values, marks):
        return jax.ops.segment_sum(
            values.reshape(-1), marks.reshape(-1), num_segments=local_blocks * code_count
        )

    return jax.vmap(summed)(paired, labels).reshape(experts, local_blocks, code_count)


def local(weights, codebook, assign, chol_upper, inv_blocks):
    block_size = inv_blocks.shape[2]
    local_blocks = inv_blocks.shape[1]
    local_width = weights.shape[2]
    code_count = codebook.shape[3]
    column_rank = lax.axis_index("col")
    block_total = local_blocks * lax.axis_size("col")
    labels = flat_labels(assign, block_size // 2, code_count)
    quantized = lookup_local(codebook, labels)
    column_ids = column_rank * local_width + jnp.arange(local_width, dtype=jnp.int32)
    stacked = lax.all_gather(chol_upper, "row", axis=1, tiled=True)

    def panel_of(number):
        return lax.dynamic_slice_in_dim(stacked, number * block_size, block_size, 1)

    def own_block(current, number):
        return lax.dynamic_slice_in_dim(current, number % local_blocks * block_size, block_size, 2)

    def block_error(current_block, number):
        owner_rank = number // local_blocks
        inverse = lax.dynamic_index_in_dim(inv_blocks, number % local_blocks, 1, keepdims=False)
        target = own_block(quantized, number)

        def compute():
            return jnp.einsum(
                "xrc,xcd->xrd", current_block - target, inverse, precision=lax.Precision.HIGHEST
            )

        def nothing():
            return jnp.zeros(current_block.shape, jnp.float32)

        computed = lax.cond(owner_rank == column_rank, compute, nothing)
        return from_root(computed, "col", owner_rank)

    def propagate(current, error_block, panel_rows, number, targets):
        beyond = targets >= (number + 1) * block_size
        masked = jnp.where(beyond[None, None, :], panel_rows, 0.0)
        return current - jnp.einsum(
            "xrc,xcd->xrd", error_block, masked, precision=lax.Precision.HIGHEST
        )

    def record(errors, error_block, number):
        owner_rank = number // local_blocks
        offset = number % local_blocks * block_size
        previous = lax.dynamic_slice_in_dim(errors, offset, block_size, 2)
        chosen = jnp.where(owner_rank == column_rank, error_block, previous)
        return lax.dynamic_update_slice_in_dim(errors, chosen, offset, 2)

    blank = jnp.zeros(weights.shape, jnp.float32)

    def advance(number, state_pair):
        current, errors = state_pair
        error_block = block_error(own_block(current, number), number)
        errors = record(errors, error_block, number)
        current = propagate(current, error_block, panel_of(number), number, column_ids)
        return (current, errors)

    current, errors = lax.fori_loop(0, block_total, advance, (weights, blank))
    row_loss = lax.psum(jnp.sum(errors * errors, axis=2), "col")
    local_mass = mass_by_code(errors, labels, local_blocks, code_count)
    codeword_mass = lax.psum(local_mass, "row")
    return (errors, row_loss, codeword_mass)


def solution(mesh):
    return jax.shard_map(
        local,
        mesh=mesh,
        in_specs=(
            P("ea", "row", "col"),
            P("ea", "col", None, None),
            P("ea", "row", "col"),
            P("ea", "row", "col"),
            P("ea", "col", None, None),
        ),
        out_specs=(P("ea", "row", "col"), P("ea", "row"), P("ea", "col", None)),
        check_vma=False,
    )
```

profile of v0, /device:TPU:0, one launch (start us, length us, event | category | flops | bytes accessed | tf_op | source)
XLA Modules:
  0.0 742.4 jit_solution(10534728693327028452)
XLA Ops:
  9.9 190.2 %gather_fusion.1 = f32[32768]{0:T(1024)S(1)} fusion(f32[1,2048]{1,0:T(1,128)S(1)} %get-tuple-element.332, s32[32768]{0:T(1024)S(1)} %bitcast.50), kind=kCustom, calls=%fused_computation.1.clone | custom fusion | bytes 524288 | tf_op jit(solution)/shard_map/vmap(jit(_take))/gather | solution.py:24
  200.2 190.2 %gather_fusion = f32[32768]{0:T(1024)S(1)} fusion(f32[1,2048]{1,0:T(1,128)S(1)} %get-tuple-element.333, s32[32768]{0:T(1024)S(1)} %bitcast.51), kind=kCustom, calls=%fused_computation.clone | custom fusion | bytes 524288 | tf_op jit(solution)/shard_map/vmap(jit(_take))/gather | solution.py:24
  392.2 98.7 %while.18 = (s32[]{:T(128)}, f32[1,64,1024]{2,1,0:T(8,128)S(1)}, f32[1,64,1024]{2,1,0:T(8,128)S(1)}, s32[]{:T(128)}, f32[1,64,1024]{2,1,0:T(8,128)S(1)}, /*index...) while((s32[]{:T(128)}, f32[1,64,1024]{2,1,0:T(8,128)S(1)}, ...), condition=%wide.region_4.6_spmd.clone, body=%wide.region_0.5_spmd.clone.sunk | while | flops 113477664 | bytes 1477659 | solution.py:101
  392.3 1.1 conditional.3
  393.4 3.4 psum.32
  396.8 1.5 fusion.35
  398.4 1.1 conditional.3
  398.4 1.1 convolution_bitcast_fusion
  399.6 3.4 psum.32
  403.0 1.5 fusion.35
  404.6 1.1 conditional.3
  404.6 1.1 convolution_bitcast_fusion
  405.7 3.4 psum.32
  409.1 1.5 fusion.35
  410.7 1.1 conditional.3
  411.9 3.4 psum.32
  415.3 1.5 fusion.35
  416.9 1.1 conditional.3
  418.0 3.4 psum.32
  421.4 1.5 fusion.35
  423.1 1.1 conditional.3
  424.2 3.4 psum.32
  427.6 1.5 fusion.35
  429.2 1.1 conditional.3
  430.3 3.4 psum.32
  433.8 1.5 fusion.35
  435.4 1.1 conditional.3
  436.5 3.4 psum.32
  439.9 1.5 fusion.35
  441.6 4.6 psum.32
  446.2 1.5 fusion.35
  447.9 4.5 psum.32
  452.4 1.5 fusion.35
  454.1 4.5 psum.32
  458.5 1.5 fusion.35
  460.2 4.5 psum.32
  464.7 1.5 fusion.35
  466.4 4.5 psum.32
  470.9 1.5 fusion.35
  472.5 4.5 psum.32
  477.0 1.5 fusion.35
  478.7 4.5 psum.32
  483.2 1.5 fusion.35
  484.8 4.5 psum.32
  489.3 1.5 fusion.35
  491.0 3.0 psum.28
  495.0 226.3 %scatter_custom_fusion = f32[2048]{0:T(1024)S(1)} fusion(s32[32768]{0:T(1024)S(1)} %broadcast_select_fusion.1, f32[32768]{0:T(1024)S(1)} %bitcast.55, f32[]{:T(128)} %constant.181.clone.1), kind=kCustom, calls=%fused_computation.45 | custom fusion | flops 32768 | bytes 8196
  721.4 14.2 %psum.29 = f32[1,8,256]{2,1,0:T(8,128)} all-reduce(f32[1,8,256]{2,1,0:T(8,128)S(1)} %reshape.106), channel_id=1, replica_groups=mesh['ea'=4,'row'=4,'col'=2] {'row'}, use_global_device_ids=true, to_apply=%region_9.11 | all-reduce | flops 2048 | bytes 16384 | tf_op jit(solution)/shard_map/psum | solution.py:104
  (105 shorter events, 12.7 us)
Async XLA Ops:
  7.2 385.0 %all-gather.2.cloned.1.call-start = ((), (), s32[]{:S(2)}) async-start(), calls=%async_computation | async-start | bytes 10485760 | tf_op jit(solution)/shard_map/all_gather | solution.py:54
  200.2 190.9 %copy-start.3 = (s32[2]{0:T(128)S(1)}, s32[2]{0:T(128)}, u32[]{:S(2)}) copy-start(s32[2]{0:T(128)} %constant.194) | copy-start | bytes 28
  200.2 191.3 %copy-start.2 = (s32[2]{0:T(128)S(1)}, s32[2]{0:T(128)}, u32[]{:S(2)}) copy-start(s32[2]{0:T(128)} %constant.197) | copy-start | bytes 28
  200.2 192.0 %copy-start = (f32[1,64,1024]{2,1,0:T(8,128)S(1)}, f32[1,64,1024]{2,1,0:T(8,128)}, u32[]{:S(2)}) copy-start(f32[1,64,1024]{2,1,0:T(8,128)} %param.11) | copy-start | bytes 786436
  490.9 244.6 %copy-start.1 = (f32[1,64,1024]{2,1,0:T(8,128)}, f32[1,64,1024]{2,1,0:T(8,128)S(1)}, u32[]{:S(2)}) copy-start(f32[1,64,1024]{2,1,0:T(8,128)S(1)} %get-tuple-element.263) | copy-start | bytes 786436
Sparse Core Ops, SparseCore 0:
  9.5 152.3 all-gather.1
where the time goes:
time: 744 us; the launch traced here: 742 us
  local copies, waits for them, and re-layouts  382 us (51%)
  other arithmetic  230 us (31%)
  blocking collectives  80.4 us (11%)
  matrix products  33.1 us (4%)
  between operations  14.3 us (2%)
    unnamed x5, other arithmetic  227 us
    gather x3, local copies, waits for them, and re-layouts, select(): jnp.take(rows_table[0], indices)  190 us
    gather x2, local copies, waits for them, and re-layouts, select(): jnp.take(rows_table[1], indices)  190 us
    psum x16, blocking collectives, from_root(): return lax.psum(kept, axis)  63.3 us
    dot_general x16, matrix products, propagate(): jnp.einsum('xrc,xcd->xrd', error_block, masked, precision=lax.Precision.H...  24.4 us
  transfers between devices with their start and end apart: 1, of which 0 were waited for; matrix products, arithmetic and copies ran while one was open for 52% of the time, Pallas kernels for 0%

commit v1 on v0

--- a/solution.py
+++ b/solution.py
@@ -1,44 +1,103 @@
 import jax
 import jax.numpy as jnp
 from jax import lax
+from jax.experimental import pallas as pl
+from jax.experimental.pallas import tpu as pltpu
 from jax.sharding import PartitionSpec as P
+
+LANES = 128
+RADIX = 16
+VMEM = pl.BlockSpec(memory_space=pltpu.VMEM)
+
+
+def lane_take(values, index):
+    return jnp.take_along_axis(values, index, axis=1, mode="promise_in_bounds")
+
+
+def expanded_codes(codes, half, rows):
+    lane = lax.broadcasted_iota(jnp.int32, (rows, LANES), 1)
+    return lane_take(codes, half * (LANES // 2) + lane // 2)
+
+
+def difference_kernel(weights_ref, codebook_ref, assign_ref, out_ref):
+    rows = weights_ref.shape[0]
+    blocks, _, code_count = codebook_ref.shape
+    odd = lax.broadcasted_iota(jnp.int32, (rows, LANES), 1) % 2 == 1
+    for block in range(blocks):
+        lanes = pl.ds(block * LANES, LANES)
+        pairs = assign_ref[:, pl.ds(block // 2 * LANES, LANES)]
+        code = expanded_codes(pairs, block % 2, rows)
+        low = code % LANES
+        page = code // LANES
+        found = jnp.zeros((rows, LANES), jnp.float32)
+        for part in range(code_count // LANES):
+            span = pl.ds(part * LANES, LANES)
+            picked = [
+                lane_take(jnp.broadcast_to(codebook_ref[block, k : k + 1, span], (rows, LANES)), low)
+                for k in range(2)
+            ]
+            found = jnp.where(page == part, jnp.where(odd, picked[1], picked[0]), found)
+        out_ref[:, lanes] = weights_ref[:, lanes] - found
+
+
+def mass_kernel(errors_ref, assign_ref, out_ref, left, right):
+    rows = errors_ref.shape[0]
+    blocks = out_ref.shape[0]
+    digits = out_ref.shape[1]
+    for block in range(blocks):
+        err = errors_ref[:, pl.ds(block * LANES, LANES)]
+        value = err * err
+        upper = value.astype(jnp.bfloat16).astype(jnp.float32)
+        lower = value - upper
+        code = expanded_codes(assign_ref[:, pl.ds(block // 2 * LANES, LANES)], block % 2, rows)
+        high = code // RADIX
+        low = code % RADIX
+        digit = lax.broadcasted_iota(jnp.int32, (digits, LANES), 0)
+        digit_low = lax.broadcasted_iota(jnp.int32, (RADIX, LANES), 0)
+        for row in range(rows):
+            one = slice(row, row + 1)
+            lanes = pl.ds(row * LANES, LANES)
+            hit = jnp.broadcast_to(high[one], (digits, LANES)) == digit
+            left[0:digits, lanes] = jnp.where(hit, jnp.broadcast_to(upper[one], hit.shape), 0.0).astype(jnp.bfloat16)
+            left[digits:, lanes] = jnp.where(hit, jnp.broadcast_to(lower[one], hit.shape), 0.0).astype(jnp.bfloat16)
+            match = jnp.broadcast_to(low[one], (RADIX, LANES)) == digit_low
+            right[:, lanes] = jnp.where(match, 1.0, 0.0).astype(jnp.bfloat16)
+        both = lax.dot_general(
+            left[...], right[...], (((1,), (1,)), ((), ())), preferred_element_type=jnp.float32
+        )
+        out_ref[block] = both[:digits] + both[digits:]
+
+
+def difference(weights, codebook, assign):
+    return pl.pallas_call(
+        difference_kernel,
+        out_shape=jax.ShapeDtypeStruct(weights.shape, jnp.float32),
+        in_specs=[VMEM] * 3,
+        out_specs=VMEM,
+        name="difference",
+    )(weights, codebook, assign)
+
+
+def local_mass(errors, assign, code_count):
+    rows, width = errors.shape
+    digits = code_count // RADIX
+    out = pl.pallas_call(
+        mass_kernel,
+        out_shape=jax.ShapeDtypeStruct((width // LANES, digits, RADIX), jnp.float32),
+        in_specs=[VMEM] * 2,
+        out_specs=VMEM,
+        scratch_shapes=[
+            pltpu.VMEM((2 * digits, rows * LANES), jnp.bfloat16),
+            pltpu.VMEM((RADIX, rows * LANES), jnp.bfloat16),
+        ],
+        name="mass",
+    )(errors, assign)
+    return out.reshape(width // LANES, code_count)
 
 
 def from_root(value, axis, source):
     kept = jnp.where(lax.axis_index(axis) == source, value, 0).astype(value.dtype)
     return lax.psum(kept, axis)
-
-
-def flat_labels(assign, half_block, code_count):
-    pair_count = assign.shape[2]
-    offsets = jnp.arange(pair_count, dtype=jnp.int32) // half_block * code_count
-    return assign + offsets[None, None, :]
-
-
-def lookup_local(codebook, labels):
-    experts, row_count, pair_count = labels.shape
-    code_table = jnp.transpose(codebook, (0, 2, 1, 3)).reshape(experts, 2, -1)
-
-    def select(rows_table, indices):
-        return jnp.stack(
-            [jnp.take(rows_table[0], indices), jnp.take(rows_table[1], indices)], axis=-1
-        )
-
-    picked = jax.vmap(select)(code_table, labels)
-    return picked.reshape(experts, row_count, 2 * pair_count)
-
-
-def mass_by_code(errors, labels, local_blocks, code_count):
-    experts, row_count, width = errors.shape
-    squared = errors * errors
-    paired = squared.reshape(experts, row_count, width // 2, 2).sum(axis=3)
-
-    def summed(values, marks):
-        return jax.ops.segment_sum(
-            values.reshape(-1), marks.reshape(-1), num_segments=local_blocks * code_count
-        )
-
-    return jax.vmap(summed)(paired, labels).reshape(experts, local_blocks, code_count)
 
 
 def local(weights, codebook, assign, chol_upper, inv_blocks):
@@ -48,8 +107,7 @@
     code_count = codebook.shape[3]
     column_rank = lax.axis_index("col")
     block_total = local_blocks * lax.axis_size("col")
-    labels = flat_labels(assign, block_size // 2, code_count)
-    quantized = lookup_local(codebook, labels)
+    offset_weights = difference(weights[0], codebook[0], assign[0])[None]
     column_ids = column_rank * local_width + jnp.arange(local_width, dtype=jnp.int32)
     stacked = lax.all_gather(chol_upper, "row", axis=1, tiled=True)
 
@@ -62,11 +120,10 @@
     def block_error(current_block, number):
         owner_rank = number // local_blocks
         inverse = lax.dynamic_index_in_dim(inv_blocks, number % local_blocks, 1, keepdims=False)
-        target = own_block(quantized, number)
 
         def compute():
             return jnp.einsum(
-                "xrc,xcd->xrd", current_block - target, inverse, precision=lax.Precision.HIGHEST
+                "xrc,xcd->xrd", current_block, inverse, precision=lax.Precision.HIGHEST
             )
 
         def nothing():
@@ -98,10 +155,10 @@
         current = propagate(current, error_block, panel_of(number), number, column_ids)
         return (current, errors)
 
-    current, errors = lax.fori_loop(0, block_total, advance, (weights, blank))
+    current, errors = lax.fori_loop(0, block_total, advance, (offset_weights, blank))
     row_loss = lax.psum(jnp.sum(errors * errors, axis=2), "col")
-    local_mass = mass_by_code(errors, labels, local_blocks, code_count)
-    codeword_mass = lax.psum(local_mass, "row")
+    mass = local_mass(errors[0], assign[0], code_count)[None]
+    codeword_mass = lax.psum(mass, "row")
     return (errors, row_loss, codeword_mass)
 
 

time: 744 us -> 288 us (0.39)
  local copies, waits for them, and re-layouts: 382 us -> 0.98 us
  other arithmetic: 230 us -> 0.61 us
  waiting for transfers between devices: 0.7 us -> 152 us
  Pallas kernels: 0 us -> 7.81 us
    gather x5 -> x0, local copies, waits for them, and re-layouts: 381 us -> none  [the longest x3 190 us: select(): jnp.take(rows_table[0], indices)]
    unnamed x5 -> x0, other arithmetic: 227 us -> none
    all_gather x1, waiting for transfers between devices: 0.02 us -> 152 us  [local(): stacked = lax.all_gather(chol_upper, 'row', axis=1, tiled=True)]
    pallas_call x0 -> x2, Pallas kernels: none -> 7.81 us  [the longest x1 5.5 us: local_mass(): pl.pallas_call(mass_kernel, out_shape=jax.ShapeDtypeStruct((width // LANE...]
  transfers between devices with their start and end apart: 1 -> 1, of which waited for: 0 -> 1; matrix products, arithmetic and copies ran while one was open for 52% -> 0% of each run, Pallas kernels for 0% -> 1%
where the time goes in v1:
time: 288 us; the launch traced here: 286 us
  waiting for transfers between devices  152 us (53%)
  blocking collectives  75.7 us (26%)
  matrix products  33.1 us (11%)
  between operations  14.1 us (5%)
  Pallas kernels  7.81 us (3%)
    all_gather x1, waiting for transfers between devices, local(): stacked = lax.all_gather(chol_upper, 'row', axis=1, tiled=True)  152 us
    psum x16, blocking collectives, from_root(): return lax.psum(kept, axis)  63.3 us
    dot_general x16, matrix products, propagate(): jnp.einsum('xrc,xcd->xrd', error_block, masked, precision=lax.Precision.H...  24.4 us
    psum x1, blocking collectives, local(): codeword_mass = lax.psum(mass, 'row')  9.38 us
    dot_general x8, matrix products, compute(): jnp.einsum('xrc,xcd->xrd', current_block, inverse, precision=lax.Precisio...  8.68 us
  transfers between devices with their start and end apart: 1, of which 1 were waited for; matrix products, arithmetic and copies ran while one was open for 0% of the time, Pallas kernels for 1%

profile of v1, /device:TPU:0, one launch (start us, length us, event | category | flops | bytes accessed | tf_op | source)
XLA Modules:
  0.0 286.4 jit_solution(15816435583354001246)
XLA Ops:
  7.9 2.3 difference.1
  10.2 151.7 %all-gather.2.cloned.1.call-done = f32[1,2048,1024]{2,1,0:T(8,128)} async-done(((f32[1,512,1024]{2,1,0:T(8,128)}), f32[1,2048,1024]{2,1,0:T(8,128)}) %all-gather.2.cloned.1.call-update) | async-done | bytes 8388624 | tf_op jit(solution)/shard_map/all_gather | solution.py:112
  161.9 98.7 %while.18 = (s32[]{:T(128)}, f32[1,64,1024]{2,1,0:T(8,128)S(1)}, f32[1,64,1024]{2,1,0:T(8,128)S(1)}, s32[]{:T(128)}, f32[1,8,128,128]{3,2,1,0:T(8,128)}, /*index...) while((s32[]{:T(128)}, f32[1,64,1024]{2,1,0:T(8,128)S(1)}, ...), condition=%wide.region_4.5_spmd.clone, body=%wide.region_0.4_spmd.clone.sunk | while | flops 113469472 | bytes 1444875 | solution.py:158
  162.0 1.1 conditional.3
  163.1 3.4 %psum.32 = f32[1,64,128]{2,1,0:T(8,128)S(1)} all-reduce(f32[1,64,128]{2,1,0:T(8,128)S(1)} %broadcast_select_fusion.2), channel_id=1, replica_groups=mesh['ea'=4,'row'=4,'col'=2] {'col'}, use_global_device_ids=true, to_apply=%region_3.3 | all-reduce | flops 8192 | bytes 65536 | tf_op jit(solution)/shard_map/while/body/eval_jaxpr/psum | solution.py:100
  166.5 1.5 fusion.21
  168.1 1.1 conditional.3
  169.3 3.4 %psum.32 = f32[1,64,128]{2,1,0:T(8,128)S(1)} all-reduce(f32[1,64,128]{2,1,0:T(8,128)S(1)} %broadcast_select_fusion.2), channel_id=1, replica_groups=mesh['ea'=4,'row'=4,'col'=2] {'col'}, use_global_device_ids=true, to_apply=%region_3.3 | all-reduce | flops 8192 | bytes 65536 | tf_op jit(solution)/shard_map/while/body/eval_jaxpr/psum | solution.py:100
  172.7 1.5 fusion.21
  174.3 1.1 conditional.3
  174.3 1.1 convolution_bitcast_fusion
  175.4 3.4 %psum.32 = f32[1,64,128]{2,1,0:T(8,128)S(1)} all-reduce(f32[1,64,128]{2,1,0:T(8,128)S(1)} %broadcast_select_fusion.2), channel_id=1, replica_groups=mesh['ea'=4,'row'=4,'col'=2] {'col'}, use_global_device_ids=true, to_apply=%region_3.3 | all-reduce | flops 8192 | bytes 65536 | tf_op jit(solution)/shard_map/while/body/eval_jaxpr/psum | solution.py:100
  178.9 1.5 fusion.21
  180.5 1.1 conditional.3
  180.5 1.1 convolution_bitcast_fusion
  181.6 3.4 %psum.32 = f32[1,64,128]{2,1,0:T(8,128)S(1)} all-reduce(f32[1,64,128]{2,1,0:T(8,128)S(1)} %broadcast_select_fusion.2), channel_id=1, replica_groups=mesh['ea'=4,'row'=4,'col'=2] {'col'}, use_global_device_ids=true, to_apply=%region_3.3 | all-reduce | flops 8192 | bytes 65536 | tf_op jit(solution)/shard_map/while/body/eval_jaxpr/psum | solution.py:100
  185.0 1.5 fusion.21
  186.6 1.1 conditional.3
  187.8 3.4 %psum.32 = f32[1,64,128]{2,1,0:T(8,128)S(1)} all-reduce(f32[1,64,128]{2,1,0:T(8,128)S(1)} %broadcast_select_fusion.2), channel_id=1, replica_groups=mesh['ea'=4,'row'=4,'col'=2] {'col'}, use_global_device_ids=true, to_apply=%region_3.3 | all-reduce | flops 8192 | bytes 65536 | tf_op jit(solution)/shard_map/while/body/eval_jaxpr/psum | solution.py:100
  191.2 1.5 fusion.21
  192.8 1.1 conditional.3
  193.9 3.4 %psum.32 = f32[1,64,128]{2,1,0:T(8,128)S(1)} all-reduce(f32[1,64,128]{2,1,0:T(8,128)S(1)} %broadcast_select_fusion.2), channel_id=1, replica_groups=mesh['ea'=4,'row'=4,'col'=2] {'col'}, use_global_device_ids=true, to_apply=%region_3.3 | all-reduce | flops 8192 | bytes 65536 | tf_op jit(solution)/shard_map/while/body/eval_jaxpr/psum | solution.py:100
  197.3 1.5 fusion.21
  198.9 1.1 conditional.3
  200.1 3.4 %psum.32 = f32[1,64,128]{2,1,0:T(8,128)S(1)} all-reduce(f32[1,64,128]{2,1,0:T(8,128)S(1)} %broadcast_select_fusion.2), channel_id=1, replica_groups=mesh['ea'=4,'row'=4,'col'=2] {'col'}, use_global_device_ids=true, to_apply=%region_3.3 | all-reduce | flops 8192 | bytes 65536 | tf_op jit(solution)/shard_map/while/body/eval_jaxpr/psum | solution.py:100
  203.5 1.5 fusion.21
  205.1 1.1 conditional.3
  206.2 3.4 %psum.32 = f32[1,64,128]{2,1,0:T(8,128)S(1)} all-reduce(f32[1,64,128]{2,1,0:T(8,128)S(1)} %broadcast_select_fusion.2), channel_id=1, replica_groups=mesh['ea'=4,'row'=4,'col'=2] {'col'}, use_global_device_ids=true, to_apply=%region_3.3 | all-reduce | flops 8192 | bytes 65536 | tf_op jit(solution)/shard_map/while/body/eval_jaxpr/psum | solution.py:100
  209.6 1.5 fusion.21
  211.3 4.7 %psum.32 = f32[1,64,128]{2,1,0:T(8,128)S(1)} all-reduce(f32[1,64,128]{2,1,0:T(8,128)S(1)} %broadcast_select_fusion.2), channel_id=1, replica_groups=mesh['ea'=4,'row'=4,'col'=2] {'col'}, use_global_device_ids=true, to_apply=%region_3.3 | all-reduce | flops 8192 | bytes 65536 | tf_op jit(solution)/shard_map/while/body/eval_jaxpr/psum | solution.py:100
  216.0 1.5 fusion.21
  217.6 4.5 %psum.32 = f32[1,64,128]{2,1,0:T(8,128)S(1)} all-reduce(f32[1,64,128]{2,1,0:T(8,128)S(1)} %broadcast_select_fusion.2), channel_id=1, replica_groups=mesh['ea'=4,'row'=4,'col'=2] {'col'}, use_global_device_ids=true, to_apply=%region_3.3 | all-reduce | flops 8192 | bytes 65536 | tf_op jit(solution)/shard_map/while/body/eval_jaxpr/psum | solution.py:100
  222.1 1.5 fusion.21
  223.8 4.5 %psum.32 = f32[1,64,128]{2,1,0:T(8,128)S(1)} all-reduce(f32[1,64,128]{2,1,0:T(8,128)S(1)} %broadcast_select_fusion.2), channel_id=1, replica_groups=mesh['ea'=4,'row'=4,'col'=2] {'col'}, use_global_device_ids=true, to_apply=%region_3.3 | all-reduce | flops 8192 | bytes 65536 | tf_op jit(solution)/shard_map/while/body/eval_jaxpr/psum | solution.py:100
  228.3 1.5 fusion.21
  230.0 4.5 %psum.32 = f32[1,64,128]{2,1,0:T(8,128)S(1)} all-reduce(f32[1,64,128]{2,1,0:T(8,128)S(1)} %broadcast_select_fusion.2), channel_id=1, replica_groups=mesh['ea'=4,'row'=4,'col'=2] {'col'}, use_global_device_ids=true, to_apply=%region_3.3 | all-reduce | flops 8192 | bytes 65536 | tf_op jit(solution)/shard_map/while/body/eval_jaxpr/psum | solution.py:100
  234.4 1.5 fusion.21
  236.1 4.5 %psum.32 = f32[1,64,128]{2,1,0:T(8,128)S(1)} all-reduce(f32[1,64,128]{2,1,0:T(8,128)S(1)} %broadcast_select_fusion.2), channel_id=1, replica_groups=mesh['ea'=4,'row'=4,'col'=2] {'col'}, use_global_device_ids=true, to_apply=%region_3.3 | all-reduce | flops 8192 | bytes 65536 | tf_op jit(solution)/shard_map/while/body/eval_jaxpr/psum | solution.py:100
  240.6 1.5 fusion.21
  242.3 4.5 %psum.32 = f32[1,64,128]{2,1,0:T(8,128)S(1)} all-reduce(f32[1,64,128]{2,1,0:T(8,128)S(1)} %broadcast_select_fusion.2), channel_id=1, replica_groups=mesh['ea'=4,'row'=4,'col'=2] {'col'}, use_global_device_ids=true, to_apply=%region_3.3 | all-reduce | flops 8192 | bytes 65536 | tf_op jit(solution)/shard_map/while/body/eval_jaxpr/psum | solution.py:100
  246.8 1.5 fusion.21
  248.4 4.5 %psum.32 = f32[1,64,128]{2,1,0:T(8,128)S(1)} all-reduce(f32[1,64,128]{2,1,0:T(8,128)S(1)} %broadcast_select_fusion.2), channel_id=1, replica_groups=mesh['ea'=4,'row'=4,'col'=2] {'col'}, use_global_device_ids=true, to_apply=%region_3.3 | all-reduce | flops 8192 | bytes 65536 | tf_op jit(solution)/shard_map/while/body/eval_jaxpr/psum | solution.py:100
  252.9 1.5 fusion.21
  254.6 4.5 %psum.32 = f32[1,64,128]{2,1,0:T(8,128)S(1)} all-reduce(f32[1,64,128]{2,1,0:T(8,128)S(1)} %broadcast_select_fusion.2), channel_id=1, replica_groups=mesh['ea'=4,'row'=4,'col'=2] {'col'}, use_global_device_ids=true, to_apply=%region_3.3 | all-reduce | flops 8192 | bytes 65536 | tf_op jit(solution)/shard_map/while/body/eval_jaxpr/psum | solution.py:100
  259.1 1.5 fusion.21
  260.8 3.0 %psum.28 = f32[1,64]{1,0:T(1,128)} all-reduce(f32[1,64]{1,0:T(1,128)S(1)} %bitcast.36), channel_id=1, replica_groups=mesh['ea'=4,'row'=4,'col'=2] {'col'}, use_global_device_ids=true, to_apply=%region_6.7 | all-reduce | flops 64 | bytes 512 | tf_op jit(solution)/shard_map/psum | solution.py:159
  263.8 5.5 %mass.1 = f32[8,16,16]{2,1,0:T(8,128)} custom-call(f32[64,1024]{1,0:T(8,128)S(1)} %bitcast.31, s32[64,512]{1,0:T(8,128)} %bitcast.33), custom_call_target="tpu_custom_call" | custom-call | tf_op jit(solution)/shard_map/mass/pallas_call | solution.py:84
  270.2 9.4 %psum.29 = f32[1,8,256]{2,1,0:T(8,128)} all-reduce(f32[1,8,256]{2,1,0:T(8,128)S(1)} %broadcast_in_dim_reshape.3), channel_id=1, replica_groups=mesh['ea'=4,'row'=4,'col'=2] {'row'}, use_global_device_ids=true, to_apply=%region_7.8 | all-reduce | flops 2048 | bytes 16384 | tf_op jit(solution)/shard_map/psum | solution.py:161
  (77 shorter events, 9.0 us)
Async XLA Ops:
  7.2 154.7 %all-gather.2.cloned.1.call-start = ((), (), s32[]{:S(2)}) async-start(), calls=%async_computation | async-start | bytes 10485760 | tf_op jit(solution)/shard_map/all_gather | solution.py:112
  260.7 18.9 %copy-start = (f32[1,64,1024]{2,1,0:T(8,128)}, f32[1,64,1024]{2,1,0:T(8,128)S(1)}, u32[]{:S(2)}) copy-start(f32[1,64,1024]{2,1,0:T(8,128)S(1)} %get-tuple-element.230) | copy-start | bytes 786436
Sparse Core Ops, SparseCore 0:
  9.5 152.3 all-gather.1

commit v2 on v1

--- a/solution.py
+++ b/solution.py
@@ -1,3 +1,4 @@
+import functools
 import jax
 import jax.numpy as jnp
 from jax import lax
@@ -10,6 +11,13 @@
 VMEM = pl.BlockSpec(memory_space=pltpu.VMEM)
 
 
+def params(flops=0, nbytes=0, limit=16):
+    return dict(
+        compiler_params=pltpu.CompilerParams(vmem_limit_bytes=limit * 2**20),
+        cost_estimate=pl.CostEstimate(flops=flops, bytes_accessed=nbytes, transcendentals=0),
+    )
+
+
 def lane_take(values, index):
     return jnp.take_along_axis(values, index, axis=1, mode="promise_in_bounds")
 
@@ -19,7 +27,20 @@
     return lane_take(codes, half * (LANES // 2) + lane // 2)
 
 
-def difference_kernel(weights_ref, codebook_ref, assign_ref, out_ref):
+def difference_kernel(weights_hbm, codebook_hbm, assign_hbm, *refs):
+    weights_ref, codebook_ref, assign_ref, sems = refs[-4:]
+    out_refs = refs[:-4]
+    copies = [
+        pltpu.make_async_copy(src, dst, sems.at[n])
+        for n, (src, dst) in enumerate(
+            [(codebook_hbm, codebook_ref), (assign_hbm, assign_ref), (weights_hbm, weights_ref)]
+        )
+    ]
+    for copy in copies:
+        copy.start()
+    for copy in copies:
+        copy.wait()
+    span = out_refs[0].shape[1]
     rows = weights_ref.shape[0]
     blocks, _, code_count = codebook_ref.shape
     odd = lax.broadcasted_iota(jnp.int32, (rows, LANES), 1) % 2 == 1
@@ -31,16 +52,17 @@
         page = code // LANES
         found = jnp.zeros((rows, LANES), jnp.float32)
         for part in range(code_count // LANES):
-            span = pl.ds(part * LANES, LANES)
+            page_lanes = pl.ds(part * LANES, LANES)
             picked = [
-                lane_take(jnp.broadcast_to(codebook_ref[block, k : k + 1, span], (rows, LANES)), low)
+                lane_take(jnp.broadcast_to(codebook_ref[block, k : k + 1, page_lanes], (rows, LANES)), low)
                 for k in range(2)
             ]
             found = jnp.where(page == part, jnp.where(odd, picked[1], picked[0]), found)
-        out_ref[:, lanes] = weights_ref[:, lanes] - found
-
-
-def mass_kernel(errors_ref, assign_ref, out_ref, left, right):
+        place = block * LANES
+        out_refs[place // span][:, pl.ds(place % span, LANES)] = weights_ref[:, lanes] - found
+
+
+def mass_kernel(errors_ref, assign_ref, out_ref, left, right, first=0):
     rows = errors_ref.shape[0]
     blocks = out_ref.shape[0]
     digits = out_ref.shape[1]
@@ -49,7 +71,8 @@
         value = err * err
         upper = value.astype(jnp.bfloat16).astype(jnp.float32)
         lower = value - upper
-        code = expanded_codes(assign_ref[:, pl.ds(block // 2 * LANES, LANES)], block % 2, rows)
+        number = first + block
+        code = expanded_codes(assign_ref[:, pl.ds(number // 2 * LANES, LANES)], number % 2, rows)
         high = code // RADIX
         low = code % RADIX
         digit = lax.broadcasted_iota(jnp.int32, (digits, LANES), 0)
@@ -68,13 +91,21 @@
         out_ref[block] = both[:digits] + both[digits:]
 
 
-def difference(weights, codebook, assign):
+def difference(weights, codebook, assign, pieces):
+    rows, width = weights.shape
     return pl.pallas_call(
         difference_kernel,
-        out_shape=jax.ShapeDtypeStruct(weights.shape, jnp.float32),
-        in_specs=[VMEM] * 3,
-        out_specs=VMEM,
+        out_shape=[jax.ShapeDtypeStruct((rows, width // pieces), jnp.float32)] * pieces,
+        in_specs=[pl.BlockSpec(memory_space=pltpu.HBM)] * 3,
+        out_specs=[VMEM] * pieces,
+        scratch_shapes=[
+            pltpu.VMEM(weights.shape, weights.dtype),
+            pltpu.VMEM(codebook.shape, codebook.dtype),
+            pltpu.VMEM(assign.shape, assign.dtype),
+            pltpu.SemaphoreType.DMA((3,)),
+        ],
         name="difference",
+        **params(64 * rows * width, 12 * rows * width, 62),
     )(weights, codebook, assign)
 
 
@@ -95,19 +126,271 @@
     return out.reshape(width // LANES, code_count)
 
 
+def halves(value):
+    upper = value.astype(jnp.bfloat16)
+    return upper, (value - upper.astype(jnp.float32)).astype(jnp.bfloat16)
+
+
+def dot32(a, b):
+    return jnp.dot(a, b, preferred_element_type=jnp.float32)
+
+
+def dot_split(a, b_upper, b_lower):
+    upper, lower = halves(a)
+    return dot32(upper, b_upper) + (dot32(upper, b_lower) + dot32(lower, b_upper))
+
+
+def factor_kernel(first_chip, last_chip, chips, own_chol, other_chol, own_inv, other_inv, *refs):
+    out, (work, blocks, sems) = refs[:-3], refs[-3:]
+    span = own_chol.shape[0]
+    count = span // LANES
+    per = own_chol.shape[1] // span
+    chip, mine = lax.axis_index("row"), lax.axis_index("col")
+    place, wanted = lax.rem(chip, per), lax.div(chip, per)
+    diagonal = pl.ds(pl.multiple_of(place * span, span), span)
+    inv_at = pl.ds(place * count, count)
+
+    def transfer(source, target, sem, chosen):
+        def start():
+            for src, condition in zip(source, (chosen, jnp.logical_not(chosen))):
+                @pl.when(condition)
+                def _():
+                    pltpu.make_async_copy(src, target, sem).start()
+
+        return start, pltpu.make_async_copy(source[0], target, sem).wait
+
+    @pl.when((chip >= first_chip) & (chip <= last_chip))
+    def _():
+        here = mine == wanted
+        first = [
+            transfer((own_inv.at[inv_at], other_inv.at[inv_at]), blocks, sems.at[0], here),
+            transfer((own_chol.at[:, diagonal], other_chol.at[:, diagonal]), work.at[0], sems.at[1], here),
+        ]
+        panels = {}
+        for t in range(first_chip + 1, chips):
+            columns = pl.ds(t % per * span, span)
+            source = (own_chol.at[:, columns], other_chol.at[:, columns])
+            panels[t] = transfer(source, work.at[t], sems.at[t + 1], mine == t // per)
+        for start, _ in first:
+            start()
+        for t, (start, _) in panels.items():
+            pl.when(t > chip)(start)
+        for _, wait in first:
+            wait()
+        inverse = work.at[chips]
+        inverse[...] = jnp.zeros((span, span), jnp.float32)
+        for b in range(count):
+            at = pl.ds(b * LANES, LANES)
+            inverse[at, at] = blocks[b]
+        width = LANES
+        while width < span:
+            for begin in range(0, span, 2 * width):
+                near, beyond = pl.ds(begin, width), pl.ds(begin + width, width)
+                left = dot_split(inverse[near, near], *halves(work[0, near, beyond]))
+                inverse[near, beyond] = -dot_split(left, *halves(inverse[beyond, beyond]))
+            width *= 2
+        out[0][0], out[0][1] = halves(inverse[...])
+        for t, (_, wait) in panels.items():
+            @pl.when(t > chip)
+            def _():
+                wait()
+                out[t][0], out[t][1] = halves(work[t])
+
+
+def factors(first_chip, last_chip, chips, chol, other_chol, inverses, other_inverses):
+    span, width = chol.shape
+    count = span // LANES
+    return pl.pallas_call(
+        functools.partial(factor_kernel, first_chip, last_chip, chips),
+        out_shape=[jax.ShapeDtypeStruct((2, span, span), jnp.bfloat16)] * chips,
+        in_specs=[pl.BlockSpec(memory_space=pltpu.HBM)] * 4,
+        out_specs=[VMEM] * chips,
+        scratch_shapes=[
+            pltpu.VMEM((chips + 1, span, span), jnp.float32),
+            pltpu.VMEM((count, LANES, LANES), jnp.float32),
+            pltpu.SemaphoreType.DMA((chips + 1,)),
+        ],
+        **params(8 * span**3, 24 * span * width, 16),
+    )(chol, other_chol, inverses, other_inverses)
+
+
+def solve_kernel(pieces, offsets, bases, panels, *refs):
+    inputs = pieces + len(offsets) + len(bases)
+    rest = jnp.concatenate([ref[...] for ref in refs[:pieces]], axis=0)
+    factor = refs[inputs : inputs + 1 + panels]
+    out = refs[inputs + 1 + panels :]
+    span = rest.shape[1]
+    for ref, at in zip(refs[pieces:], offsets):
+        rest = rest - ref[:, pl.ds(at, span)]
+    err = dot_split(rest, factor[0][0], factor[0][1])
+    out[0][...] = err
+    upper, lower = halves(err)
+    for n in range(panels):
+        panel = factor[n + 1]
+        product = dot32(upper, panel[0]) + (dot32(upper, panel[1]) + dot32(lower, panel[0]))
+        for which, at in bases:
+            if which[0] == n:
+                product = product + refs[which[1]][:, pl.ds(at, span)]
+        out[1][:, pl.ds(n * span, span)] = product
+
+
+def solve(pieces, sums, bases, factor, panels):
+    rows = sum(p.shape[0] for p in pieces)
+    span = pieces[0].shape[1]
+    operands = [*pieces, *(array for array, _ in sums)]
+    marks = []
+    for n, (array, at) in bases:
+        marks.append(((n, len(operands)), at))
+        operands.append(array)
+    operands += [factor[t] for t in (0, *panels)]
+    shapes = [jax.ShapeDtypeStruct((rows, span), jnp.float32)]
+    if panels:
+        shapes.append(jax.ShapeDtypeStruct((rows, len(panels) * span), jnp.float32))
+    return pl.pallas_call(
+        functools.partial(solve_kernel, len(pieces), [at for _, at in sums], marks, len(panels)),
+        out_shape=shapes,
+        in_specs=[VMEM] * len(operands),
+        out_specs=[VMEM] * len(shapes),
+        **params(6 * rows * span * span * (1 + len(panels)), 8 * rows * span),
+    )(*operands)
+
+
+def spread_kernel(err_ref, panel, *refs):
+    total = dot_split(err_ref[...], panel[0], panel[1])
+    for ref in refs[:-1]:
+        total = total + ref[...]
+    refs[-1][...] = total
+
+
+def spread(err, panel, bases):
+    rows, span = err.shape
+    return pl.pallas_call(
+        spread_kernel,
+        out_shape=jax.ShapeDtypeStruct((rows, span), jnp.float32),
+        in_specs=[VMEM] * (2 + len(bases)),
+        out_specs=VMEM,
+        **params(6 * rows * span * span, 8 * rows * span),
+    )(err, panel, *bases)
+
+
+def finish_kernel(returned, first, assign_ref, *refs):
+    total = refs[0][...]
+    for ref in refs[1:returned]:
+        total = total + ref[...]
+    left, right = refs[-2:]
+    errors_ref, loss_ref, mass_ref = refs[-5:-2]
+    errors_ref[...] = total
+    loss_ref[...] = jnp.sum(total * total, axis=1, keepdims=True)
+    mass_kernel(errors_ref, assign_ref, mass_ref, left, right, first)
+
+
+def finish(assign, returned, first, code_count):
+    rows, span = returned[0].shape
+    digits = code_count // RADIX
+    return pl.pallas_call(
+        functools.partial(finish_kernel, len(returned), first),
+        out_shape=[
+            jax.ShapeDtypeStruct((rows, span), jnp.float32),
+            jax.ShapeDtypeStruct((rows, 1), jnp.float32),
+            jax.ShapeDtypeStruct((span // LANES, digits, RADIX), jnp.float32),
+        ],
+        in_specs=[VMEM] * (1 + len(returned)),
+        out_specs=[VMEM] * 3,
+        scratch_shapes=[
+            pltpu.VMEM((2 * digits, rows * LANES), jnp.bfloat16),
+            pltpu.VMEM((RADIX, rows * LANES), jnp.bfloat16),
+        ],
+        **params(4 * 16 * 32 * rows * span, 8 * rows * span),
+    )(assign, *returned)
+
+
+def chained(weights, codebook, assign, chol_upper, inv_blocks):
+    chips = lax.axis_size("row")
+    z = lax.axis_index("row")
+    rows, width = weights.shape[1:]
+    span = chol_upper.shape[1]
+    per = width // span
+    each = chips // 2
+    code_count = codebook.shape[3]
+    assign = assign[0]
+
+    def send(value, pairs):
+        return lax.ppermute(value, ("row", "col"), [(a * 2 + b, p * 2 + q) for (a, b), (p, q) in pairs])
+
+    def swapped(value):
+        return send(value, [((n, q), (n, 1 - q)) for n in range(chips) for q in range(2)])
+
+    def forward(value, j, t):
+        return send(value, [((j, n), (t, n)) for n in range(2)])
+
+    def routes(i, part):
+        return [((n * each + part, q), (q * per + i, n)) for q in range(2) for n in range(2)]
+
+    other_chol = swapped(chol_upper[0])
+    other_inv = swapped(inv_blocks[0])
+    local = difference(weights[0], codebook[0], assign, per)
+    arrived = {
+        (i, part): send(local[i], routes(i, part)) for i in range(per) for part in range(each)
+    }
+    halves_held = (chol_upper[0], other_chol, inv_blocks[0], other_inv)
+    factor = factors(0, chips - 1, chips, *halves_held)
+
+    incoming = {}
+    solved = {}
+    for j in range(chips):
+        first = list(range(j + 1, min(chips, j + 2 + (j == 0))))
+        outs = solve(
+            [arrived[j % per, part] for part in range(each)],
+            [incoming[j]] if j in incoming else [],
+            [(n, incoming[t]) for n, t in enumerate(first) if t in incoming],
+            factor,
+            first,
+        )
+        solved[j] = outs[0]
+        sent = {}
+        if first:
+            moved = forward(outs[1], j, j + 1)
+            sent = {t: (moved, n * span) for n, t in enumerate(first)}
+        for t in range(j + 1 + len(first), chips):
+            product = spread(outs[0], factor[t], [incoming[t][0]] if t in incoming else [])
+            sent[t] = (forward(product, j, j + 1), 0)
+        incoming = sent
+
+    errors, losses, masses = [], [], []
+    for i in range(per):
+        chosen = jnp.where(z == i, solved[i], solved[per + i])
+        returned = []
+        for part in range(each):
+            value = lax.slice_in_dim(chosen, part * rows, (part + 1) * rows, axis=0)
+            returned.append(send(value, [(b, a) for a, b in routes(i, part)]))
+        total, loss, mass = finish(assign, returned, i * span // LANES, code_count)
+        errors.append(total)
+        losses.append(loss)
+        masses.append(mass)
+    loss = sum(losses[1:], losses[0])[:, 0]
+    loss = loss + swapped(loss)
+    mass = jnp.concatenate(masses, axis=0).reshape(-1, code_count)
+    step = 1
+    while step < chips:
+        pairs = [((n, q), (n ^ step, q)) for n in range(chips) for q in range(2)]
+        mass = mass + send(mass, pairs)
+        step *= 2
+    return jnp.concatenate(errors, axis=1)[None], loss[None], mass[None]
+
+
 def from_root(value, axis, source):
     kept = jnp.where(lax.axis_index(axis) == source, value, 0).astype(value.dtype)
     return lax.psum(kept, axis)
 
 
-def local(weights, codebook, assign, chol_upper, inv_blocks):
+def general(weights, codebook, assign, chol_upper, inv_blocks):
     block_size = inv_blocks.shape[2]
     local_blocks = inv_blocks.shape[1]
     local_width = weights.shape[2]
     code_count = codebook.shape[3]
     column_rank = lax.axis_index("col")
     block_total = local_blocks * lax.axis_size("col")
-    offset_weights = difference(weights[0], codebook[0], assign[0])[None]
+    offset_weights = difference(weights[0], codebook[0], assign[0], 1)[0][None]
     column_ids = column_rank * local_width + jnp.arange(local_width, dtype=jnp.int32)
     stacked = lax.all_gather(chol_upper, "row", axis=1, tiled=True)
 
@@ -155,11 +438,26 @@
         current = propagate(current, error_block, panel_of(number), number, column_ids)
         return (current, errors)
 
-    current, errors = lax.fori_loop(0, block_total, advance, (offset_weights, blank))
+    _, errors = lax.fori_loop(0, block_total, advance, (offset_weights, blank))
     row_loss = lax.psum(jnp.sum(errors * errors, axis=2), "col")
     mass = local_mass(errors[0], assign[0], code_count)[None]
     codeword_mass = lax.psum(mass, "row")
     return (errors, row_loss, codeword_mass)
+
+
+def local(weights, codebook, assign, chol_upper, inv_blocks):
+    count = chol_upper.shape[1] // LANES
+    chips = lax.axis_size("row")
+    if (
+        lax.axis_size("col") == 2
+        and chol_upper.shape[1] == count * LANES
+        and count & (count - 1) == 0
+        and chips & (chips - 1) == 0
+        and chips > 1
+        and chips * chol_upper.shape[1] == 2 * weights.shape[2]
+    ):
+        return chained(weights, codebook, assign, chol_upper, inv_blocks)
+    return general(weights, codebook, assign, chol_upper, inv_blocks)
 
 
 def solution(mesh):

time: 288 us -> 83 us (0.29)
  waiting for transfers between devices: 152 us -> 20.7 us
  blocking collectives: 75.7 us -> 0 us
  starting transfers between devices: 0.04 us -> 42.3 us
  matrix products: 33.1 us -> 0 us
  between operations: 14.1 us -> 0.9 us
  Pallas kernels: 7.81 us -> 13.9 us
    all_gather x1 -> x0, waiting for transfers between devices: 152 us -> none  [local(): stacked = lax.all_gather(chol_upper, 'row', axis=1, tiled=True)]
    psum x18 -> x0, blocking collectives: 75.7 us -> none  [the longest x16 63.3 us: from_root(): return lax.psum(kept, axis)]
    ppermute x0 -> x18, starting transfers between devices: none -> 42.3 us  [send(): lax.ppermute(value, ('row', 'col'), [(a * 2 + b, p * 2 + q) for (a, b), (...]
    dot_general x24 -> x0, matrix products: 33.1 us -> none  [the longest x16 24.4 us: propagate(): jnp.einsum('xrc,xcd->xrd', error_block, masked, precision=lax.Precision.H...]
    ppermute x0 -> x18, waiting for transfers between devices: none -> 20.7 us  [send(): lax.ppermute(value, ('row', 'col'), [(a * 2 + b, p * 2 + q) for (a, b), (...]
    pallas_call x2 -> x10, Pallas kernels: 7.81 us -> 13.9 us  [the longest x4 4.4 us: solve(): pl.pallas_call(functools.partial(solve_kernel, len(pieces), [at for _, at...]
  transfers between devices with their start and end apart: 1 -> 18, of which waited for: 1 -> 5; matrix products, arithmetic and copies ran while one was open for 0% -> 2% of each run, Pallas kernels for 1% -> 11%
where the time goes in v2:
time: 83 us; the launch traced here: 82.6 us
  starting transfers between devices  42.3 us (51%)
  waiting for transfers between devices  20.7 us (25%)
  Pallas kernels  13.9 us (17%)
  local copies, waits for them, and re-layouts  2.76 us (3%)
  other arithmetic  2.05 us (2%)
  between operations  0.9 us (1%)
    ppermute x18, starting transfers between devices, send(): lax.ppermute(value, ('row', 'col'), [(a * 2 + b, p * 2 + q) for (a, b), (...  42.3 us
    ppermute x18, waiting for transfers between devices, send(): lax.ppermute(value, ('row', 'col'), [(a * 2 + b, p * 2 + q) for (a, b), (...  20.7 us
    pallas_call x4, Pallas kernels, solve(): pl.pallas_call(functools.partial(solve_kernel, len(pieces), [at for _, at...  4.4 us
    pallas_call x2, Pallas kernels, finish(): pl.pallas_call(functools.partial(finish_kernel, len(returned), first), ou...  3.57 us
    pallas_call x1, Pallas kernels, difference(): pl.pallas_call(difference_kernel, out_shape=[jax.ShapeDtypeStruct((rows,...  3.03 us
    unnamed x8, local copies, waits for them, and re-layouts  2.64 us
    pallas_call x1, Pallas kernels, factors(): pl.pallas_call(functools.partial(factor_kernel, first_chip, last_chip, ch...  2.13 us
    broadcast_in_dim x3, other arithmetic, chained(): return (jnp.concatenate(errors, axis=1)[None], loss[None], mass[None])  1.83 us
  transfers between devices with their start and end apart: 18, of which 5 were waited for; matrix products, arithmetic and copies ran while one was open for 2% of the time, Pallas kernels for 11%

profile of v2, /device:TPU:0, one launch (start us, length us, event | category | flops | bytes accessed | tf_op | source)
XLA Modules:
  0.0 82.6 jit_solution(253195521873089536)
XLA Ops:
  0.6 0.6 collective-permute-start.2
  1.2 0.1 collective-permute-start.3
  1.3 3.0 %difference.1 = (f32[64,512]{1,0:T(8,128)}, f32[64,512]{1,0:T(8,128)}) custom-call(f32[64,1024]{1,0:T(8,128)} %bitcast.18, f32[8,2,256]{2,1,0:T(2,128)} %bitcast.19, s32[64,512]{1,0:T(8,128)} %bitcast.13), custom_call_target="tpu_custom_call" | custom-call | flops 4194304 | bytes 786432 | tf_op jit(solution)/shard_map/difference/pallas_call | solution.py:96
  4.3 1.6 %collective-permute-start = (f32[64,512]{1,0:T(8,128)}, f32[64,512]{1,0:T(8,128)S(1)}, u32[]{:S(2)}, u32[]{:S(2)}) collective-permute-start(f32[64,512]{1,0:T(8,128)} %get-tuple-element.21), channel_id=1, source_target_pairs={{0,0},{4,1},{1,4},{5,5},{8,8},{12,9},{9,12},{13,13},{16,16},{20,17... | collective-permute-start | bytes 393224 | tf_op jit(solution)/shard_map/ppermute | solution.py:318
  5.9 1.3 %collective-permute-start.1 = (f32[64,512]{1,0:T(8,128)}, f32[64,512]{1,0:T(8,128)S(1)}, u32[]{:S(2)}, u32[]{:S(2)}) collective-permute-start(f32[64,512]{1,0:T(8,128)} %get-tuple-element.21), channel_id=1, source_target_pairs={{2,0},{6,1},{3,4},{7,5},{10,8},{14,9},{11,12},{15,13},{18,16},{22,... | collective-permute-start | bytes 393224 | tf_op jit(solution)/shard_map/ppermute | solution.py:318
  7.2 0.0 collective-permute-done.2.other_chol
  7.2 0.0 copy-start
  7.2 1.6 %copy-done = f32[1,512,1024]{2,1,0:T(8,128)S(1)} copy-done((f32[1,512,1024]{2,1,0:T(8,128)S(1)}, f32[1,512,1024]{2,1,0:T(8,128)}, u32[]{:S(2)}) %copy-start) | copy-done | bytes 2097176
  8.8 1.0 %copy-done.2 = f32[1,8,128,128]{3,2,1,0:T(8,128)S(1)} copy-done((f32[1,8,128,128]{3,2,1,0:T(8,128)S(1)}, f32[1,8,128,128]{3,2,1,0:T(8,128)}, u32[]{:S(2)}) %copy-start.2) | copy-done | bytes 524312
  9.8 2.1 %shard_map.76 = (bf16[2,512,512]{2,1,0:T(8,128)(2,1)S(1)}, bf16[2,512,512]{2,1,0:T(8,128)(2,1)S(1)}, bf16[2,512,512]{2,1,0:T(8,128)(2,1)S(1)}, bf16[2,512,512]{2,1,0:T(8,128)(2,1)S(1)}) custom-call(f32[512,1024]{1,0:T(8,128)S(1)} %bitcast.12, f32[512,1024]{1,0:T(8,128)} %collective-permute-done.2.other_chol, f32[8,128,128]{2,1,0:T(8,128)S(1)} %bitcast.17, ...), custom_call_target="tpu_custom_call" | custom-call | flops 1073741824 | bytes 12582912 | tf_op jit(solution)/shard_map/pallas_call | solution.py:203
  12.0 0.0 collective-permute-done.refs_0_
  12.0 2.4 %collective-permute-done.1.refs_1_ = f32[64,512]{1,0:T(8,128)S(1)} collective-permute-done((f32[64,512]{1,0:T(8,128)}, f32[64,512]{1,0:T(8,128)S(1)}, u32[]{:S(2)}, u32[]{:S(2)}) %collective-permute-start.1) | collective-permute-done | bytes 131104 | tf_op jit(solution)/shard_map/ppermute | solution.py:318
  14.3 0.9 %shard_map.77 = (f32[128,512]{1,0:T(8,128)S(1)}, f32[128,1024]{1,0:T(8,128)S(1)}) custom-call(f32[64,512]{1,0:T(8,128)S(1)} %collective-permute-done.refs_0_, f32[64,512]{1,0:T(8,128)S(1)} %collective-permute-done.1.refs_1_, bf16[2,512,512]{2,1,0:T(8,128)(2,1)S(1)} %get-tuple-element.22.refs_2_.refs_4_.refs_3_, ...), custom_call_target="tpu_custom_call" | custom-call | flops 603979776 | bytes 524288 | tf_op jit(solution)/shard_map/pallas_call | solution.py:249
  15.2 2.0 %collective-permute-start.6 = (f32[128,1024]{1,0:T(8,128)S(1)}, f32[128,1024]{1,0:T(8,128)S(1)}, u32[]{:S(2)}, u32[]{:S(2)}) collective-permute-start(f32[128,1024]{1,0:T(8,128)S(1)} %get-tuple-element.27), channel_id=1, source_target_pairs={{0,2},{1,3},{8,10},{9,11},{16,18},{17,19},{24,26},{25,27}} | collective-permute-start | bytes 1572872 | tf_op jit(solution)/shard_map/ppermute | solution.py:318
  17.3 0.4 shard_map.79
  17.7 1.3 %collective-permute-start.8 = (f32[128,512]{1,0:T(8,128)S(1)}, f32[128,512]{1,0:T(8,128)S(1)}, u32[]{:S(2)}, u32[]{:S(2)}) collective-permute-start(f32[128,512]{1,0:T(8,128)S(1)} %shard_map.79), channel_id=1, source_target_pairs={{0,2},{1,3},{8,10},{9,11},{16,18},{17,19},{24,26},{25,27}} | collective-permute-start | bytes 786440 | tf_op jit(solution)/shard_map/ppermute | solution.py:318
  19.0 1.3 %collective-permute-start.4 = (f32[64,512]{1,0:T(8,128)S(1)}, f32[64,512]{1,0:T(8,128)S(1)}, u32[]{:S(2)}, u32[]{:S(2)}) collective-permute-start(f32[64,512]{1,0:T(8,128)S(1)} %copy-done.3), channel_id=1, source_target_pairs={{0,2},{4,3},{1,6},{5,7},{8,10},{12,11},{9,14},{13,15},{16,18},{20,... | collective-permute-start | bytes 393224 | tf_op jit(solution)/shard_map/ppermute | solution.py:318
  20.3 0.7 collective-permute-start.5
  21.0 14.1 %collective-permute-done.4.refs_0_ = f32[64,512]{1,0:T(8,128)S(1)} collective-permute-done((f32[64,512]{1,0:T(8,128)S(1)}, f32[64,512]{1,0:T(8,128)S(1)}, u32[]{:S(2)}, u32[]{:S(2)}) %collective-permute-start.4) | collective-permute-done | bytes 131104 | tf_op jit(solution)/shard_map/ppermute | solution.py:318
  35.1 0.0 collective-permute-done.5.refs_1_
  35.1 1.4 %shard_map.78 = (f32[128,512]{1,0:T(8,128)S(1)}, f32[128,512]{1,0:T(8,128)}) custom-call(f32[64,512]{1,0:T(8,128)S(1)} %collective-permute-done.4.refs_0_, f32[64,512]{1,0:T(8,128)S(1)} %collective-permute-done.5.refs_1_, f32[128,1024]{1,0:T(8,128)S(1)} %collective-permute-done.6.refs_2_.refs_3_, f32[128,1024]{1,0:T(8,128)S(1)} %collective-permute-done.6.refs_2_.refs_3_, ...), custom_call_target="tpu_custom_call" | custom-call | flops 402653184 | bytes 524288 | tf_op jit(solution)/shard_map/pallas_call | solution.py:249
  36.5 0.0 collective-permute-done.8.refs_0_
  36.5 0.4 shard_map.80
  36.9 1.4 %collective-permute-start.9 = (f32[128,512]{1,0:T(8,128)S(1)}, f32[128,512]{1,0:T(8,128)}, u32[]{:S(2)}, u32[]{:S(2)}) collective-permute-start(f32[128,512]{1,0:T(8,128)S(1)} %shard_map.80), channel_id=1, source_target_pairs={{2,4},{3,5},{10,12},{11,13},{18,20},{19,21},{26,28},{27,29}} | collective-permute-start | bytes 786440 | tf_op jit(solution)/shard_map/ppermute | solution.py:318
  38.3 1.4 %collective-permute-start.7 = (f32[128,512]{1,0:T(8,128)}, f32[128,512]{1,0:T(8,128)}, u32[]{:S(2)}, u32[]{:S(2)}) collective-permute-start(f32[128,512]{1,0:T(8,128)} %get-tuple-element.28), channel_id=1, source_target_pairs={{2,4},{3,5},{10,12},{11,13},{18,20},{19,21},{26,28},{27,29}} | collective-permute-start | bytes 786440 | tf_op jit(solution)/shard_map/ppermute | solution.py:318
  39.6 0.0 collective-permute-done.9.refs_3_
  39.6 0.0 collective-permute-done.7.refs_2_
  39.6 1.7 %shard_map.81 = (f32[128,512]{1,0:T(8,128)S(1)}, f32[128,512]{1,0:T(8,128)S(1)}) custom-call(f32[64,512]{1,0:T(8,128)S(1)} %collective-permute-done.refs_0_, f32[64,512]{1,0:T(8,128)S(1)} %collective-permute-done.1.refs_1_, f32[128,512]{1,0:T(8,128)} %collective-permute-done.7.refs_2_, f32[128,512]{1,0:T(8,128)} %collective-permute-done.9.refs_3_, ...), custom_call_target="tpu_custom_call" | custom-call | flops 402653184 | bytes 524288 | tf_op jit(solution)/shard_map/pallas_call | solution.py:249
  41.4 0.7 collective-permute-start.12
  42.1 0.0 copy-start.1
  42.1 0.7 collective-permute-start.10
  42.8 14.5 %collective-permute-start.11 = (f32[64,512]{1,0:T(8,128)S(1)}, f32[64,512]{1,0:T(8,128)S(1)}, u32[]{:S(2)}, u32[]{:S(2)}) collective-permute-start(f32[64,512]{1,0:T(8,128)S(1)} %get-tuple-element.39), channel_id=1, source_target_pairs={{0,2},{1,6},{4,3},{5,7},{8,10},{9,14},{12,11},{13,15},{16,18},{17,... | collective-permute-start | bytes 393224 | tf_op jit(solution)/shard_map/ppermute | solution.py:318
  57.4 0.4 shard_map.83
  57.9 1.3 %collective-permute-start.13 = (f32[64,512]{1,0:T(8,128)S(1)}, f32[64,512]{1,0:T(8,128)S(1)}, u32[]{:S(2)}, u32[]{:S(2)}) collective-permute-start(f32[64,512]{1,0:T(8,128)S(1)} %get-tuple-element.42), channel_id=1, source_target_pairs={{2,0},{3,4},{6,1},{7,5},{10,8},{11,12},{14,9},{15,13},{18,16},{19,... | collective-permute-start | bytes 393224 | tf_op jit(solution)/shard_map/ppermute | solution.py:318
  59.2 0.7 collective-permute-start.14
  59.8 0.1 collective-permute-done.11.refs_1_
  60.0 1.8 %shard_map.82 = (f32[64,512]{1,0:T(8,128)S(1)}, f32[64,1]{1,0:T(8,128)S(1)}, f32[4,16,16]{2,1,0:T(8,128)S(1)}) custom-call(s32[64,512]{1,0:T(8,128)S(1)} %bitcast.14, f32[64,512]{1,0:T(8,128)S(1)} %collective-permute-done.10.refs_0_, f32[64,512]{1,0:T(8,128)S(1)} %collective-permute-done.11.refs_1_), custom_call_target="tpu_custom_call" | custom-call | flops 67108864 | bytes 262144 | tf_op jit(solution)/shard_map/pallas_call | solution.py:290
  61.7 3.0 %collective-permute-done.13.refs_0_ = f32[64,512]{1,0:T(8,128)S(1)} collective-permute-done((f32[64,512]{1,0:T(8,128)S(1)}, f32[64,512]{1,0:T(8,128)S(1)}, u32[]{:S(2)}, u32[]{:S(2)}) %collective-permute-start.13) | collective-permute-done | bytes 131104 | tf_op jit(solution)/shard_map/ppermute | solution.py:318
  64.7 1.8 %shard_map.84 = (f32[64,512]{1,0:T(8,128)S(1)}, f32[64,1]{1,0:T(8,128)S(1)}, f32[4,16,16]{2,1,0:T(8,128)S(1)}) custom-call(s32[64,512]{1,0:T(8,128)S(1)} %bitcast.15, f32[64,512]{1,0:T(8,128)S(1)} %collective-permute-done.13.refs_0_, f32[64,512]{1,0:T(8,128)S(1)} %collective-permute-done.14.refs_1_), custom_call_target="tpu_custom_call" | custom-call | flops 67108864 | bytes 262144 | tf_op jit(solution)/shard_map/pallas_call | solution.py:290
  66.5 0.1 reshape.9
  66.6 0.1 collective-permute-start.16
  66.7 0.1 add_reduce_fusion
  66.8 9.3 %collective-permute-start.15 = (f32[64]{0:T(128)S(1)}, f32[64]{0:T(128)S(1)}, u32[]{:S(2)}, u32[]{:S(2)}) collective-permute-start(f32[64]{0:T(128)S(1)} %add_reduce_fusion), channel_id=1, source_target_pairs={{0,1},{1,0},{2,3},{3,2},{4,5},{5,4},{6,7},{7,6},{8,9},{9,8},{10,11... | collective-permute-start | bytes 776 | tf_op jit(solution)/shard_map/ppermute | solution.py:318
  76.1 0.7 maximum_bitcast_fusion
  76.8 3.5 %collective-permute-start.17 = (f32[8,256]{1,0:T(8,128)S(1)}, f32[8,256]{1,0:T(8,128)S(1)}, u32[]{:S(2)}, u32[]{:S(2)}) collective-permute-start(f32[8,256]{1,0:T(8,128)S(1)} %add.14), channel_id=1, source_target_pairs={{0,4},{1,5},{2,6},{3,7},{4,0},{5,1},{6,2},{7,3},{8,12},{9,13},{10,... | collective-permute-start | bytes 24584 | tf_op jit(solution)/shard_map/ppermute | solution.py:318
  80.4 0.5 add_bitcast_fusion.1
  80.9 1.1 %collective-permute-done.17 = f32[8,256]{1,0:T(8,128)S(1)} collective-permute-done((f32[8,256]{1,0:T(8,128)S(1)}, f32[8,256]{1,0:T(8,128)S(1)}, u32[]{:S(2)}, u32[]{:S(2)}) %collective-permute-start.17) | collective-permute-done | bytes 8224 | tf_op jit(solution)/shard_map/ppermute | solution.py:318
  82.0 0.6 add_bitcast_fusion
  (17 shorter events, 0.2 us)
Async XLA Ops:
  0.6 6.5 %collective-permute-start.2 = (f32[512,1024]{1,0:T(8,128)}, f32[512,1024]{1,0:T(8,128)}, u32[]{:S(2)}, u32[]{:S(2)}) collective-permute-start(f32[512,1024]{1,0:T(8,128)} %bitcast.11), channel_id=1, source_target_pairs={{0,1},{1,0},{2,3},{3,2},{4,5},{5,4},{6,7},{7,6},{8,9},{9,8},{10,11... | collective-permute-start | bytes 6291464 | tf_op jit(solution)/shard_map/ppermute | solution.py:318
  1.2 6.0 %collective-permute-start.3 = (f32[8,128,128]{2,1,0:T(8,128)}, f32[8,128,128]{2,1,0:T(8,128)S(1)}, u32[]{:S(2)}, u32[]{:S(2)}) collective-permute-start(f32[8,128,128]{2,1,0:T(8,128)} %bitcast.16), channel_id=1, source_target_pairs={{0,1},{1,0},{2,3},{3,2},{4,5},{5,4},{6,7},{7,6},{8,9},{9,8},{10,11... | collective-permute-start | bytes 1572872 | tf_op jit(solution)/shard_map/ppermute | solution.py:318
  4.3 7.7 %collective-permute-start = (f32[64,512]{1,0:T(8,128)}, f32[64,512]{1,0:T(8,128)S(1)}, u32[]{:S(2)}, u32[]{:S(2)}) collective-permute-start(f32[64,512]{1,0:T(8,128)} %get-tuple-element.21), channel_id=1, source_target_pairs={{0,0},{4,1},{1,4},{5,5},{8,8},{12,9},{9,12},{13,13},{16,16},{20,17... | collective-permute-start | bytes 393224 | tf_op jit(solution)/shard_map/ppermute | solution.py:318
  5.9 8.5 %collective-permute-start.1 = (f32[64,512]{1,0:T(8,128)}, f32[64,512]{1,0:T(8,128)S(1)}, u32[]{:S(2)}, u32[]{:S(2)}) collective-permute-start(f32[64,512]{1,0:T(8,128)} %get-tuple-element.21), channel_id=1, source_target_pairs={{2,0},{6,1},{3,4},{7,5},{10,8},{14,9},{11,12},{15,13},{18,16},{22,... | collective-permute-start | bytes 393224 | tf_op jit(solution)/shard_map/ppermute | solution.py:318
  7.2 1.6 %copy-start = (f32[1,512,1024]{2,1,0:T(8,128)S(1)}, f32[1,512,1024]{2,1,0:T(8,128)}, u32[]{:S(2)}) copy-start(f32[1,512,1024]{2,1,0:T(8,128)} %param.8) | copy-start | bytes 6291460
  8.8 1.0 %copy-start.2 = (f32[1,8,128,128]{3,2,1,0:T(8,128)S(1)}, f32[1,8,128,128]{3,2,1,0:T(8,128)}, u32[]{:S(2)}) copy-start(f32[1,8,128,128]{3,2,1,0:T(8,128)} %param.9) | copy-start | bytes 1572868
  14.3 4.7 %copy-start.3 = (f32[64,512]{1,0:T(8,128)S(1)}, f32[64,512]{1,0:T(8,128)}, u32[]{:S(2)}) copy-start(f32[64,512]{1,0:T(8,128)} %get-tuple-element.26) | copy-start | bytes 393220
  15.2 19.9 %collective-permute-start.6 = (f32[128,1024]{1,0:T(8,128)S(1)}, f32[128,1024]{1,0:T(8,128)S(1)}, u32[]{:S(2)}, u32[]{:S(2)}) collective-permute-start(f32[128,1024]{1,0:T(8,128)S(1)} %get-tuple-element.27), channel_id=1, source_target_pairs={{0,2},{1,3},{8,10},{9,11},{16,18},{17,19},{24,26},{25,27}} | collective-permute-start | bytes 1572872 | tf_op jit(solution)/shard_map/ppermute | solution.py:318
  17.7 18.8 %collective-permute-start.8 = (f32[128,512]{1,0:T(8,128)S(1)}, f32[128,512]{1,0:T(8,128)S(1)}, u32[]{:S(2)}, u32[]{:S(2)}) collective-permute-start(f32[128,512]{1,0:T(8,128)S(1)} %shard_map.79), channel_id=1, source_target_pairs={{0,2},{1,3},{8,10},{9,11},{16,18},{17,19},{24,26},{25,27}} | collective-permute-start | bytes 786440 | tf_op jit(solution)/shard_map/ppermute | solution.py:318
  19.0 16.1 %collective-permute-start.4 = (f32[64,512]{1,0:T(8,128)S(1)}, f32[64,512]{1,0:T(8,128)S(1)}, u32[]{:S(2)}, u32[]{:S(2)}) collective-permute-start(f32[64,512]{1,0:T(8,128)S(1)} %copy-done.3), channel_id=1, source_target_pairs={{0,2},{4,3},{1,6},{5,7},{8,10},{12,11},{9,14},{13,15},{16,18},{20,... | collective-permute-start | bytes 393224 | tf_op jit(solution)/shard_map/ppermute | solution.py:318
  20.3 14.8 %collective-permute-start.5 = (f32[64,512]{1,0:T(8,128)S(1)}, f32[64,512]{1,0:T(8,128)S(1)}, u32[]{:S(2)}, u32[]{:S(2)}) collective-permute-start(f32[64,512]{1,0:T(8,128)S(1)} %copy-done.3), channel_id=1, source_target_pairs={{2,2},{6,3},{3,6},{7,7},{10,10},{14,11},{11,14},{15,15},{18,18},{2... | collective-permute-start | bytes 393224 | tf_op jit(solution)/shard_map/ppermute | solution.py:318
  36.9 2.7 %collective-permute-start.9 = (f32[128,512]{1,0:T(8,128)S(1)}, f32[128,512]{1,0:T(8,128)}, u32[]{:S(2)}, u32[]{:S(2)}) collective-permute-start(f32[128,512]{1,0:T(8,128)S(1)} %shard_map.80), channel_id=1, source_target_pairs={{2,4},{3,5},{10,12},{11,13},{18,20},{19,21},{26,28},{27,29}} | collective-permute-start | bytes 786440 | tf_op jit(solution)/shard_map/ppermute | solution.py:318
  38.3 1.4 %collective-permute-start.7 = (f32[128,512]{1,0:T(8,128)}, f32[128,512]{1,0:T(8,128)}, u32[]{:S(2)}, u32[]{:S(2)}) collective-permute-start(f32[128,512]{1,0:T(8,128)} %get-tuple-element.28), channel_id=1, source_target_pairs={{2,4},{3,5},{10,12},{11,13},{18,20},{19,21},{26,28},{27,29}} | collective-permute-start | bytes 786440 | tf_op jit(solution)/shard_map/ppermute | solution.py:318
  41.4 16.0 %collective-permute-start.12 = (f32[128,512]{1,0:T(8,128)S(1)}, f32[128,512]{1,0:T(8,128)S(1)}, u32[]{:S(2)}, u32[]{:S(2)}) collective-permute-start(f32[128,512]{1,0:T(8,128)S(1)} %get-tuple-element.33), channel_id=1, source_target_pairs={{4,6},{5,7},{12,14},{13,15},{20,22},{21,23},{28,30},{29,31}} | collective-permute-start | bytes 786440 | tf_op jit(solution)/shard_map/ppermute | solution.py:318
  42.1 17.9 %copy-start.1 = (s32[1,64,512]{2,1,0:T(8,128)S(1)}, s32[1,64,512]{2,1,0:T(8,128)}, u32[]{:S(2)}) copy-start(s32[1,64,512]{2,1,0:T(8,128)} %param.7) | copy-start | bytes 393220
  42.1 17.7 %collective-permute-start.10 = (f32[64,512]{1,0:T(8,128)S(1)}, f32[64,512]{1,0:T(8,128)S(1)}, u32[]{:S(2)}, u32[]{:S(2)}) collective-permute-start(f32[64,512]{1,0:T(8,128)S(1)} %get-tuple-element.40), channel_id=1, source_target_pairs={{0,0},{1,4},{4,1},{5,5},{8,8},{9,12},{12,9},{13,13},{16,16},{17,20... | collective-permute-start | bytes 393224 | tf_op jit(solution)/shard_map/ppermute | solution.py:318
  42.8 17.1 %collective-permute-start.11 = (f32[64,512]{1,0:T(8,128)S(1)}, f32[64,512]{1,0:T(8,128)S(1)}, u32[]{:S(2)}, u32[]{:S(2)}) collective-permute-start(f32[64,512]{1,0:T(8,128)S(1)} %get-tuple-element.39), channel_id=1, source_target_pairs={{0,2},{1,6},{4,3},{5,7},{8,10},{9,14},{12,11},{13,15},{16,18},{17,... | collective-permute-start | bytes 393224 | tf_op jit(solution)/shard_map/ppermute | solution.py:318
  57.9 6.9 %collective-permute-start.13 = (f32[64,512]{1,0:T(8,128)S(1)}, f32[64,512]{1,0:T(8,128)S(1)}, u32[]{:S(2)}, u32[]{:S(2)}) collective-permute-start(f32[64,512]{1,0:T(8,128)S(1)} %get-tuple-element.42), channel_id=1, source_target_pairs={{2,0},{3,4},{6,1},{7,5},{10,8},{11,12},{14,9},{15,13},{18,16},{19,... | collective-permute-start | bytes 393224 | tf_op jit(solution)/shard_map/ppermute | solution.py:318
  59.2 5.6 %collective-permute-start.14 = (f32[64,512]{1,0:T(8,128)S(1)}, f32[64,512]{1,0:T(8,128)S(1)}, u32[]{:S(2)}, u32[]{:S(2)}) collective-permute-start(f32[64,512]{1,0:T(8,128)S(1)} %get-tuple-element.41), channel_id=1, source_target_pairs={{2,2},{3,6},{6,3},{7,7},{10,10},{11,14},{14,11},{15,15},{18,18},{1... | collective-permute-start | bytes 393224 | tf_op jit(solution)/shard_map/ppermute | solution.py:318
  66.6 10.2 %collective-permute-start.16 = (f32[8,256]{1,0:T(8,128)S(1)}, f32[8,256]{1,0:T(8,128)S(1)}, u32[]{:S(2)}, u32[]{:S(2)}) collective-permute-start(f32[8,256]{1,0:T(8,128)S(1)} %reshape.9), channel_id=1, source_target_pairs={{0,2},{1,3},{2,0},{3,1},{4,6},{5,7},{6,4},{7,5},{8,10},{9,11},{10,... | collective-permute-start | bytes 24584 | tf_op jit(solution)/shard_map/ppermute | solution.py:318
  66.8 13.5 %collective-permute-start.15 = (f32[64]{0:T(128)S(1)}, f32[64]{0:T(128)S(1)}, u32[]{:S(2)}, u32[]{:S(2)}) collective-permute-start(f32[64]{0:T(128)S(1)} %add_reduce_fusion), channel_id=1, source_target_pairs={{0,1},{1,0},{2,3},{3,2},{4,5},{5,4},{6,7},{7,6},{8,9},{9,8},{10,11... | collective-permute-start | bytes 776 | tf_op jit(solution)/shard_map/ppermute | solution.py:318
  76.8 5.2 %collective-permute-start.17 = (f32[8,256]{1,0:T(8,128)S(1)}, f32[8,256]{1,0:T(8,128)S(1)}, u32[]{:S(2)}, u32[]{:S(2)}) collective-permute-start(f32[8,256]{1,0:T(8,128)S(1)} %add.14), channel_id=1, source_target_pairs={{0,4},{1,5},{2,6},{3,7},{4,0},{5,1},{6,2},{7,3},{8,12},{9,13},{10,... | collective-permute-start | bytes 24584 | tf_op jit(solution)/shard_map/ppermute | solution.py:318

commit v3 on v2

--- a/solution.py
+++ b/solution.py
@@ -38,7 +38,7 @@
     ]
     for copy in copies:
         copy.start()
-    for copy in copies:
+    for copy in copies[:2]:
         copy.wait()
     span = out_refs[0].shape[1]
     rows = weights_ref.shape[0]
@@ -58,6 +58,8 @@
                 for k in range(2)
             ]
             found = jnp.where(page == part, jnp.where(odd, picked[1], picked[0]), found)
+        if block == 0:
+            copies[2].wait()
         place = block * LANES
         out_refs[place // span][:, pl.ds(place % span, LANES)] = weights_ref[:, lanes] - found
 
@@ -370,11 +372,11 @@
     loss = sum(losses[1:], losses[0])[:, 0]
     loss = loss + swapped(loss)
     mass = jnp.concatenate(masses, axis=0).reshape(-1, code_count)
-    step = 1
-    while step < chips:
+    step = chips // 2
+    while step:
         pairs = [((n, q), (n ^ step, q)) for n in range(chips) for q in range(2)]
         mass = mass + send(mass, pairs)
-        step *= 2
+        step //= 2
     return jnp.concatenate(errors, axis=1)[None], loss[None], mass[None]
 
 

time: 83 us -> 83 us (level)
  no operation moved by 1% of the time
where the time goes in v3:
time: 83 us; the launch traced here: 82.6 us
  starting transfers between devices  42.3 us (51%)
  waiting for transfers between devices  20.7 us (25%)
  Pallas kernels  13.9 us (17%)
  local copies, waits for them, and re-layouts  2.76 us (3%)
  other arithmetic  2.05 us (2%)
  between operations  0.89 us (1%)
    ppermute x18, starting transfers between devices, send(): lax.ppermute(value, ('row', 'col'), [(a * 2 + b, p * 2 + q) for (a, b), (...  42.3 us
    ppermute x18, waiting for transfers between devices, send(): lax.ppermute(value, ('row', 'col'), [(a * 2 + b, p * 2 + q) for (a, b), (...  20.7 us
    pallas_call x4, Pallas kernels, solve(): pl.pallas_call(functools.partial(solve_kernel, len(pieces), [at for _, at...  4.4 us
    pallas_call x2, Pallas kernels, finish(): pl.pallas_call(functools.partial(finish_kernel, len(returned), first), ou...  3.57 us
    pallas_call x1, Pallas kernels, difference(): pl.pallas_call(difference_kernel, out_shape=[jax.ShapeDtypeStruct((rows,...  3.01 us
    unnamed x8, local copies, waits for them, and re-layouts  2.64 us
    pallas_call x1, Pallas kernels, factors(): pl.pallas_call(functools.partial(factor_kernel, first_chip, last_chip, ch...  2.13 us
    broadcast_in_dim x3, other arithmetic, chained(): return (jnp.concatenate(errors, axis=1)[None], loss[None], mass[None])  1.83 us
  transfers between devices with their start and end apart: 18, of which 5 were waited for; matrix products, arithmetic and copies ran while one was open for 2% of the time, Pallas kernels for 11%

profile of v3, /device:TPU:0, one launch (start us, length us, event | category | flops | bytes accessed | tf_op | source)
XLA Modules:
  0.0 82.6 jit_solution(17744074165867841077)
XLA Ops:
  0.6 0.6 collective-permute-start.2
  1.2 0.1 collective-permute-start.3
  1.3 3.0 %difference.1 = (f32[64,512]{1,0:T(8,128)}, f32[64,512]{1,0:T(8,128)}) custom-call(f32[64,1024]{1,0:T(8,128)} %bitcast.18, f32[8,2,256]{2,1,0:T(2,128)} %bitcast.19, s32[64,512]{1,0:T(8,128)} %bitcast.13), custom_call_target="tpu_custom_call" | custom-call | flops 4194304 | bytes 786432 | tf_op jit(solution)/shard_map/difference/pallas_call | solution.py:98
  4.3 1.6 %collective-permute-start = (f32[64,512]{1,0:T(8,128)}, f32[64,512]{1,0:T(8,128)S(1)}, u32[]{:S(2)}, u32[]{:S(2)}) collective-permute-start(f32[64,512]{1,0:T(8,128)} %get-tuple-element.21), channel_id=1, source_target_pairs={{0,0},{4,1},{1,4},{5,5},{8,8},{12,9},{9,12},{13,13},{16,16},{20,17... | collective-permute-start | bytes 393224 | tf_op jit(solution)/shard_map/ppermute | solution.py:320
  5.8 1.3 %collective-permute-start.1 = (f32[64,512]{1,0:T(8,128)}, f32[64,512]{1,0:T(8,128)S(1)}, u32[]{:S(2)}, u32[]{:S(2)}) collective-permute-start(f32[64,512]{1,0:T(8,128)} %get-tuple-element.21), channel_id=1, source_target_pairs={{2,0},{6,1},{3,4},{7,5},{10,8},{14,9},{11,12},{15,13},{18,16},{22,... | collective-permute-start | bytes 393224 | tf_op jit(solution)/shard_map/ppermute | solution.py:320
  7.1 0.0 collective-permute-done.3.other_inv
  7.1 0.0 collective-permute-done.2.other_chol
  7.2 0.0 copy-start
  7.2 1.6 %copy-done = f32[1,512,1024]{2,1,0:T(8,128)S(1)} copy-done((f32[1,512,1024]{2,1,0:T(8,128)S(1)}, f32[1,512,1024]{2,1,0:T(8,128)}, u32[]{:S(2)}) %copy-start) | copy-done | bytes 2097176
  8.8 1.0 %copy-done.2 = f32[1,8,128,128]{3,2,1,0:T(8,128)S(1)} copy-done((f32[1,8,128,128]{3,2,1,0:T(8,128)S(1)}, f32[1,8,128,128]{3,2,1,0:T(8,128)}, u32[]{:S(2)}) %copy-start.2) | copy-done | bytes 524312
  9.8 2.1 %shard_map.76 = (bf16[2,512,512]{2,1,0:T(8,128)(2,1)S(1)}, bf16[2,512,512]{2,1,0:T(8,128)(2,1)S(1)}, bf16[2,512,512]{2,1,0:T(8,128)(2,1)S(1)}, bf16[2,512,512]{2,1,0:T(8,128)(2,1)S(1)}) custom-call(f32[512,1024]{1,0:T(8,128)S(1)} %bitcast.12, f32[512,1024]{1,0:T(8,128)} %collective-permute-done.2.other_chol, f32[8,128,128]{2,1,0:T(8,128)S(1)} %bitcast.17, ...), custom_call_target="tpu_custom_call" | custom-call | flops 1073741824 | bytes 12582912 | tf_op jit(solution)/shard_map/pallas_call | solution.py:205
  11.9 0.0 collective-permute-done.refs_0_
  11.9 2.4 %collective-permute-done.1.refs_1_ = f32[64,512]{1,0:T(8,128)S(1)} collective-permute-done((f32[64,512]{1,0:T(8,128)}, f32[64,512]{1,0:T(8,128)S(1)}, u32[]{:S(2)}, u32[]{:S(2)}) %collective-permute-start.1) | collective-permute-done | bytes 131104 | tf_op jit(solution)/shard_map/ppermute | solution.py:320
  14.3 0.9 %shard_map.77 = (f32[128,512]{1,0:T(8,128)S(1)}, f32[128,1024]{1,0:T(8,128)S(1)}) custom-call(f32[64,512]{1,0:T(8,128)S(1)} %collective-permute-done.refs_0_, f32[64,512]{1,0:T(8,128)S(1)} %collective-permute-done.1.refs_1_, bf16[2,512,512]{2,1,0:T(8,128)(2,1)S(1)} %get-tuple-element.22.refs_2_.refs_4_.refs_3_, ...), custom_call_target="tpu_custom_call" | custom-call | flops 603979776 | bytes 524288 | tf_op jit(solution)/shard_map/pallas_call | solution.py:251
  15.2 2.0 %collective-permute-start.6 = (f32[128,1024]{1,0:T(8,128)S(1)}, f32[128,1024]{1,0:T(8,128)S(1)}, u32[]{:S(2)}, u32[]{:S(2)}) collective-permute-start(f32[128,1024]{1,0:T(8,128)S(1)} %get-tuple-element.27), channel_id=1, source_target_pairs={{0,2},{1,3},{8,10},{9,11},{16,18},{17,19},{24,26},{25,27}} | collective-permute-start | bytes 1572872 | tf_op jit(solution)/shard_map/ppermute | solution.py:320
  17.3 0.4 shard_map.79
  17.7 1.3 %collective-permute-start.8 = (f32[128,512]{1,0:T(8,128)S(1)}, f32[128,512]{1,0:T(8,128)S(1)}, u32[]{:S(2)}, u32[]{:S(2)}) collective-permute-start(f32[128,512]{1,0:T(8,128)S(1)} %shard_map.79), channel_id=1, source_target_pairs={{0,2},{1,3},{8,10},{9,11},{16,18},{17,19},{24,26},{25,27}} | collective-permute-start | bytes 786440 | tf_op jit(solution)/shard_map/ppermute | solution.py:320
  19.0 1.3 %collective-permute-start.4 = (f32[64,512]{1,0:T(8,128)S(1)}, f32[64,512]{1,0:T(8,128)S(1)}, u32[]{:S(2)}, u32[]{:S(2)}) collective-permute-start(f32[64,512]{1,0:T(8,128)S(1)} %copy-done.3), channel_id=1, source_target_pairs={{0,2},{4,3},{1,6},{5,7},{8,10},{12,11},{9,14},{13,15},{16,18},{20,... | collective-permute-start | bytes 393224 | tf_op jit(solution)/shard_map/ppermute | solution.py:320
  20.3 0.7 collective-permute-start.5
  21.0 14.1 %collective-permute-done.4.refs_0_ = f32[64,512]{1,0:T(8,128)S(1)} collective-permute-done((f32[64,512]{1,0:T(8,128)S(1)}, f32[64,512]{1,0:T(8,128)S(1)}, u32[]{:S(2)}, u32[]{:S(2)}) %collective-permute-start.4) | collective-permute-done | bytes 131104 | tf_op jit(solution)/shard_map/ppermute | solution.py:320
  35.1 0.0 collective-permute-done.5.refs_1_
  35.1 0.0 collective-permute-done.6.refs_2_.refs_3_
  35.1 1.4 %shard_map.78 = (f32[128,512]{1,0:T(8,128)S(1)}, f32[128,512]{1,0:T(8,128)}) custom-call(f32[64,512]{1,0:T(8,128)S(1)} %collective-permute-done.4.refs_0_, f32[64,512]{1,0:T(8,128)S(1)} %collective-permute-done.5.refs_1_, f32[128,1024]{1,0:T(8,128)S(1)} %collective-permute-done.6.refs_2_.refs_3_, f32[128,1024]{1,0:T(8,128)S(1)} %collective-permute-done.6.refs_2_.refs_3_, ...), custom_call_target="tpu_custom_call" | custom-call | flops 402653184 | bytes 524288 | tf_op jit(solution)/shard_map/pallas_call | solution.py:251
  36.5 0.0 collective-permute-done.8.refs_0_
  36.5 0.4 shard_map.80
  36.9 1.4 %collective-permute-start.9 = (f32[128,512]{1,0:T(8,128)S(1)}, f32[128,512]{1,0:T(8,128)}, u32[]{:S(2)}, u32[]{:S(2)}) collective-permute-start(f32[128,512]{1,0:T(8,128)S(1)} %shard_map.80), channel_id=1, source_target_pairs={{2,4},{3,5},{10,12},{11,13},{18,20},{19,21},{26,28},{27,29}} | collective-permute-start | bytes 786440 | tf_op jit(solution)/shard_map/ppermute | solution.py:320
  38.2 1.4 %collective-permute-start.7 = (f32[128,512]{1,0:T(8,128)}, f32[128,512]{1,0:T(8,128)}, u32[]{:S(2)}, u32[]{:S(2)}) collective-permute-start(f32[128,512]{1,0:T(8,128)} %get-tuple-element.28), channel_id=1, source_target_pairs={{2,4},{3,5},{10,12},{11,13},{18,20},{19,21},{26,28},{27,29}} | collective-permute-start | bytes 786440 | tf_op jit(solution)/shard_map/ppermute | solution.py:320
  39.6 1.7 %shard_map.81 = (f32[128,512]{1,0:T(8,128)S(1)}, f32[128,512]{1,0:T(8,128)S(1)}) custom-call(f32[64,512]{1,0:T(8,128)S(1)} %collective-permute-done.refs_0_, f32[64,512]{1,0:T(8,128)S(1)} %collective-permute-done.1.refs_1_, f32[128,512]{1,0:T(8,128)} %collective-permute-done.7.refs_2_, f32[128,512]{1,0:T(8,128)} %collective-permute-done.9.refs_3_, ...), custom_call_target="tpu_custom_call" | custom-call | flops 402653184 | bytes 524288 | tf_op jit(solution)/shard_map/pallas_call | solution.py:251
  41.4 0.7 collective-permute-start.12
  42.0 0.0 copy-start.1
  42.1 0.7 collective-permute-start.10
  42.8 14.6 %collective-permute-start.11 = (f32[64,512]{1,0:T(8,128)S(1)}, f32[64,512]{1,0:T(8,128)S(1)}, u32[]{:S(2)}, u32[]{:S(2)}) collective-permute-start(f32[64,512]{1,0:T(8,128)S(1)} %get-tuple-element.39), channel_id=1, source_target_pairs={{0,2},{1,6},{4,3},{5,7},{8,10},{9,14},{12,11},{13,15},{16,18},{17,... | collective-permute-start | bytes 393224 | tf_op jit(solution)/shard_map/ppermute | solution.py:320
  57.4 0.4 shard_map.83
  57.8 1.3 %collective-permute-start.13 = (f32[64,512]{1,0:T(8,128)S(1)}, f32[64,512]{1,0:T(8,128)S(1)}, u32[]{:S(2)}, u32[]{:S(2)}) collective-permute-start(f32[64,512]{1,0:T(8,128)S(1)} %get-tuple-element.42), channel_id=1, source_target_pairs={{2,0},{3,4},{6,1},{7,5},{10,8},{11,12},{14,9},{15,13},{18,16},{19,... | collective-permute-start | bytes 393224 | tf_op jit(solution)/shard_map/ppermute | solution.py:320
  59.1 0.7 collective-permute-start.14
  59.8 0.1 collective-permute-done.11.refs_1_
  59.9 1.8 %shard_map.82 = (f32[64,512]{1,0:T(8,128)S(1)}, f32[64,1]{1,0:T(8,128)S(1)}, f32[4,16,16]{2,1,0:T(8,128)S(1)}) custom-call(s32[64,512]{1,0:T(8,128)S(1)} %bitcast.14, f32[64,512]{1,0:T(8,128)S(1)} %collective-permute-done.10.refs_0_, f32[64,512]{1,0:T(8,128)S(1)} %collective-permute-done.11.refs_1_), custom_call_target="tpu_custom_call" | custom-call | flops 67108864 | bytes 262144 | tf_op jit(solution)/shard_map/pallas_call | solution.py:292
  61.7 3.0 %collective-permute-done.13.refs_0_ = f32[64,512]{1,0:T(8,128)S(1)} collective-permute-done((f32[64,512]{1,0:T(8,128)S(1)}, f32[64,512]{1,0:T(8,128)S(1)}, u32[]{:S(2)}, u32[]{:S(2)}) %collective-permute-start.13) | collective-permute-done | bytes 131104 | tf_op jit(solution)/shard_map/ppermute | solution.py:320
  64.7 1.8 %shard_map.84 = (f32[64,512]{1,0:T(8,128)S(1)}, f32[64,1]{1,0:T(8,128)S(1)}, f32[4,16,16]{2,1,0:T(8,128)S(1)}) custom-call(s32[64,512]{1,0:T(8,128)S(1)} %bitcast.15, f32[64,512]{1,0:T(8,128)S(1)} %collective-permute-done.13.refs_0_, f32[64,512]{1,0:T(8,128)S(1)} %collective-permute-done.14.refs_1_), custom_call_target="tpu_custom_call" | custom-call | flops 67108864 | bytes 262144 | tf_op jit(solution)/shard_map/pallas_call | solution.py:292
  66.5 0.1 reshape.9
  66.6 5.9 %collective-permute-start.16 = (f32[8,256]{1,0:T(8,128)S(1)}, f32[8,256]{1,0:T(8,128)S(1)}, u32[]{:S(2)}, u32[]{:S(2)}) collective-permute-start(f32[8,256]{1,0:T(8,128)S(1)} %reshape.9), channel_id=1, source_target_pairs={{0,4},{1,5},{2,6},{3,7},{4,0},{5,1},{6,2},{7,3},{8,12},{9,13},{10,... | collective-permute-start | bytes 24584 | tf_op jit(solution)/shard_map/ppermute | solution.py:320
  72.5 0.1 add_reduce_fusion
  72.6 1.2 %collective-permute-start.15 = (f32[64]{0:T(128)S(1)}, f32[64]{0:T(128)S(1)}, u32[]{:S(2)}, u32[]{:S(2)}) collective-permute-start(f32[64]{0:T(128)S(1)} %add_reduce_fusion), channel_id=1, source_target_pairs={{0,1},{1,0},{2,3},{3,2},{4,5},{5,4},{6,7},{7,6},{8,9},{9,8},{10,11... | collective-permute-start | bytes 776 | tf_op jit(solution)/shard_map/ppermute | solution.py:320
  73.9 0.7 maximum_bitcast_fusion
  74.6 5.7 %collective-permute-start.17 = (f32[8,256]{1,0:T(8,128)S(1)}, f32[8,256]{1,0:T(8,128)S(1)}, u32[]{:S(2)}, u32[]{:S(2)}) collective-permute-start(f32[8,256]{1,0:T(8,128)S(1)} %add.14), channel_id=1, source_target_pairs={{0,2},{1,3},{2,0},{3,1},{4,6},{5,7},{6,4},{7,5},{8,10},{9,11},{10,... | collective-permute-start | bytes 24584 | tf_op jit(solution)/shard_map/ppermute | solution.py:320
  80.3 0.5 add_bitcast_fusion.1
  80.9 1.1 %collective-permute-done.17 = f32[8,256]{1,0:T(8,128)S(1)} collective-permute-done((f32[8,256]{1,0:T(8,128)S(1)}, f32[8,256]{1,0:T(8,128)S(1)}, u32[]{:S(2)}, u32[]{:S(2)}) %collective-permute-start.17) | collective-permute-done | bytes 8224 | tf_op jit(solution)/shard_map/ppermute | solution.py:320
  82.0 0.6 add_bitcast_fusion
  (17 shorter events, 0.2 us)
Async XLA Ops:
  0.6 6.5 %collective-permute-start.2 = (f32[512,1024]{1,0:T(8,128)}, f32[512,1024]{1,0:T(8,128)}, u32[]{:S(2)}, u32[]{:S(2)}) collective-permute-start(f32[512,1024]{1,0:T(8,128)} %bitcast.11), channel_id=1, source_target_pairs={{0,1},{1,0},{2,3},{3,2},{4,5},{5,4},{6,7},{7,6},{8,9},{9,8},{10,11... | collective-permute-start | bytes 6291464 | tf_op jit(solution)/shard_map/ppermute | solution.py:320
  1.2 6.0 %collective-permute-start.3 = (f32[8,128,128]{2,1,0:T(8,128)}, f32[8,128,128]{2,1,0:T(8,128)S(1)}, u32[]{:S(2)}, u32[]{:S(2)}) collective-permute-start(f32[8,128,128]{2,1,0:T(8,128)} %bitcast.16), channel_id=1, source_target_pairs={{0,1},{1,0},{2,3},{3,2},{4,5},{5,4},{6,7},{7,6},{8,9},{9,8},{10,11... | collective-permute-start | bytes 1572872 | tf_op jit(solution)/shard_map/ppermute | solution.py:320
  4.3 7.7 %collective-permute-start = (f32[64,512]{1,0:T(8,128)}, f32[64,512]{1,0:T(8,128)S(1)}, u32[]{:S(2)}, u32[]{:S(2)}) collective-permute-start(f32[64,512]{1,0:T(8,128)} %get-tuple-element.21), channel_id=1, source_target_pairs={{0,0},{4,1},{1,4},{5,5},{8,8},{12,9},{9,12},{13,13},{16,16},{20,17... | collective-permute-start | bytes 393224 | tf_op jit(solution)/shard_map/ppermute | solution.py:320
  5.8 8.5 %collective-permute-start.1 = (f32[64,512]{1,0:T(8,128)}, f32[64,512]{1,0:T(8,128)S(1)}, u32[]{:S(2)}, u32[]{:S(2)}) collective-permute-start(f32[64,512]{1,0:T(8,128)} %get-tuple-element.21), channel_id=1, source_target_pairs={{2,0},{6,1},{3,4},{7,5},{10,8},{14,9},{11,12},{15,13},{18,16},{22,... | collective-permute-start | bytes 393224 | tf_op jit(solution)/shard_map/ppermute | solution.py:320
  7.2 1.6 %copy-start = (f32[1,512,1024]{2,1,0:T(8,128)S(1)}, f32[1,512,1024]{2,1,0:T(8,128)}, u32[]{:S(2)}) copy-start(f32[1,512,1024]{2,1,0:T(8,128)} %param.8) | copy-start | bytes 6291460
  8.8 1.0 %copy-start.2 = (f32[1,8,128,128]{3,2,1,0:T(8,128)S(1)}, f32[1,8,128,128]{3,2,1,0:T(8,128)}, u32[]{:S(2)}) copy-start(f32[1,8,128,128]{3,2,1,0:T(8,128)} %param.9) | copy-start | bytes 1572868
  14.3 4.7 %copy-start.3 = (f32[64,512]{1,0:T(8,128)S(1)}, f32[64,512]{1,0:T(8,128)}, u32[]{:S(2)}) copy-start(f32[64,512]{1,0:T(8,128)} %get-tuple-element.26) | copy-start | bytes 393220
  15.2 19.9 %collective-permute-start.6 = (f32[128,1024]{1,0:T(8,128)S(1)}, f32[128,1024]{1,0:T(8,128)S(1)}, u32[]{:S(2)}, u32[]{:S(2)}) collective-permute-start(f32[128,1024]{1,0:T(8,128)S(1)} %get-tuple-element.27), channel_id=1, source_target_pairs={{0,2},{1,3},{8,10},{9,11},{16,18},{17,19},{24,26},{25,27}} | collective-permute-start | bytes 1572872 | tf_op jit(solution)/shard_map/ppermute | solution.py:320
  17.7 18.8 %collective-permute-start.8 = (f32[128,512]{1,0:T(8,128)S(1)}, f32[128,512]{1,0:T(8,128)S(1)}, u32[]{:S(2)}, u32[]{:S(2)}) collective-permute-start(f32[128,512]{1,0:T(8,128)S(1)} %shard_map.79), channel_id=1, source_target_pairs={{0,2},{1,3},{8,10},{9,11},{16,18},{17,19},{24,26},{25,27}} | collective-permute-start | bytes 786440 | tf_op jit(solution)/shard_map/ppermute | solution.py:320
  19.0 16.1 %collective-permute-start.4 = (f32[64,512]{1,0:T(8,128)S(1)}, f32[64,512]{1,0:T(8,128)S(1)}, u32[]{:S(2)}, u32[]{:S(2)}) collective-permute-start(f32[64,512]{1,0:T(8,128)S(1)} %copy-done.3), channel_id=1, source_target_pairs={{0,2},{4,3},{1,6},{5,7},{8,10},{12,11},{9,14},{13,15},{16,18},{20,... | collective-permute-start | bytes 393224 | tf_op jit(solution)/shard_map/ppermute | solution.py:320
  20.3 14.8 %collective-permute-start.5 = (f32[64,512]{1,0:T(8,128)S(1)}, f32[64,512]{1,0:T(8,128)S(1)}, u32[]{:S(2)}, u32[]{:S(2)}) collective-permute-start(f32[64,512]{1,0:T(8,128)S(1)} %copy-done.3), channel_id=1, source_target_pairs={{2,2},{6,3},{3,6},{7,7},{10,10},{14,11},{11,14},{15,15},{18,18},{2... | collective-permute-start | bytes 393224 | tf_op jit(solution)/shard_map/ppermute | solution.py:320
  36.9 2.7 %collective-permute-start.9 = (f32[128,512]{1,0:T(8,128)S(1)}, f32[128,512]{1,0:T(8,128)}, u32[]{:S(2)}, u32[]{:S(2)}) collective-permute-start(f32[128,512]{1,0:T(8,128)S(1)} %shard_map.80), channel_id=1, source_target_pairs={{2,4},{3,5},{10,12},{11,13},{18,20},{19,21},{26,28},{27,29}} | collective-permute-start | bytes 786440 | tf_op jit(solution)/shard_map/ppermute | solution.py:320
  38.2 1.4 %collective-permute-start.7 = (f32[128,512]{1,0:T(8,128)}, f32[128,512]{1,0:T(8,128)}, u32[]{:S(2)}, u32[]{:S(2)}) collective-permute-start(f32[128,512]{1,0:T(8,128)} %get-tuple-element.28), channel_id=1, source_target_pairs={{2,4},{3,5},{10,12},{11,13},{18,20},{19,21},{26,28},{27,29}} | collective-permute-start | bytes 786440 | tf_op jit(solution)/shard_map/ppermute | solution.py:320
  41.4 16.0 %collective-permute-start.12 = (f32[128,512]{1,0:T(8,128)S(1)}, f32[128,512]{1,0:T(8,128)S(1)}, u32[]{:S(2)}, u32[]{:S(2)}) collective-permute-start(f32[128,512]{1,0:T(8,128)S(1)} %get-tuple-element.33), channel_id=1, source_target_pairs={{4,6},{5,7},{12,14},{13,15},{20,22},{21,23},{28,30},{29,31}} | collective-permute-start | bytes 786440 | tf_op jit(solution)/shard_map/ppermute | solution.py:320
  42.0 17.9 %copy-start.1 = (s32[1,64,512]{2,1,0:T(8,128)S(1)}, s32[1,64,512]{2,1,0:T(8,128)}, u32[]{:S(2)}) copy-start(s32[1,64,512]{2,1,0:T(8,128)} %param.7) | copy-start | bytes 393220
  42.1 17.7 %collective-permute-start.10 = (f32[64,512]{1,0:T(8,128)S(1)}, f32[64,512]{1,0:T(8,128)S(1)}, u32[]{:S(2)}, u32[]{:S(2)}) collective-permute-start(f32[64,512]{1,0:T(8,128)S(1)} %get-tuple-element.40), channel_id=1, source_target_pairs={{0,0},{1,4},{4,1},{5,5},{8,8},{9,12},{12,9},{13,13},{16,16},{17,20... | collective-permute-start | bytes 393224 | tf_op jit(solution)/shard_map/ppermute | solution.py:320
  42.8 17.1 %collective-permute-start.11 = (f32[64,512]{1,0:T(8,128)S(1)}, f32[64,512]{1,0:T(8,128)S(1)}, u32[]{:S(2)}, u32[]{:S(2)}) collective-permute-start(f32[64,512]{1,0:T(8,128)S(1)} %get-tuple-element.39), channel_id=1, source_target_pairs={{0,2},{1,6},{4,3},{5,7},{8,10},{9,14},{12,11},{13,15},{16,18},{17,... | collective-permute-start | bytes 393224 | tf_op jit(solution)/shard_map/ppermute | solution.py:320
  57.8 6.9 %collective-permute-start.13 = (f32[64,512]{1,0:T(8,128)S(1)}, f32[64,512]{1,0:T(8,128)S(1)}, u32[]{:S(2)}, u32[]{:S(2)}) collective-permute-start(f32[64,512]{1,0:T(8,128)S(1)} %get-tuple-element.42), channel_id=1, source_target_pairs={{2,0},{3,4},{6,1},{7,5},{10,8},{11,12},{14,9},{15,13},{18,16},{19,... | collective-permute-start | bytes 393224 | tf_op jit(solution)/shard_map/ppermute | solution.py:320
  59.1 5.6 %collective-permute-start.14 = (f32[64,512]{1,0:T(8,128)S(1)}, f32[64,512]{1,0:T(8,128)S(1)}, u32[]{:S(2)}, u32[]{:S(2)}) collective-permute-start(f32[64,512]{1,0:T(8,128)S(1)} %get-tuple-element.41), channel_id=1, source_target_pairs={{2,2},{3,6},{6,3},{7,7},{10,10},{11,14},{14,11},{15,15},{18,18},{1... | collective-permute-start | bytes 393224 | tf_op jit(solution)/shard_map/ppermute | solution.py:320
  66.6 8.0 %collective-permute-start.16 = (f32[8,256]{1,0:T(8,128)S(1)}, f32[8,256]{1,0:T(8,128)S(1)}, u32[]{:S(2)}, u32[]{:S(2)}) collective-permute-start(f32[8,256]{1,0:T(8,128)S(1)} %reshape.9), channel_id=1, source_target_pairs={{0,4},{1,5},{2,6},{3,7},{4,0},{5,1},{6,2},{7,3},{8,12},{9,13},{10,... | collective-permute-start | bytes 24584 | tf_op jit(solution)/shard_map/ppermute | solution.py:320
  72.6 7.7 %collective-permute-start.15 = (f32[64]{0:T(128)S(1)}, f32[64]{0:T(128)S(1)}, u32[]{:S(2)}, u32[]{:S(2)}) collective-permute-start(f32[64]{0:T(128)S(1)} %add_reduce_fusion), channel_id=1, source_target_pairs={{0,1},{1,0},{2,3},{3,2},{4,5},{5,4},{6,7},{7,6},{8,9},{9,8},{10,11... | collective-permute-start | bytes 776 | tf_op jit(solution)/shard_map/ppermute | solution.py:320
  74.6 7.4 %collective-permute-start.17 = (f32[8,256]{1,0:T(8,128)S(1)}, f32[8,256]{1,0:T(8,128)S(1)}, u32[]{:S(2)}, u32[]{:S(2)}) collective-permute-start(f32[8,256]{1,0:T(8,128)S(1)} %add.14), channel_id=1, source_target_pairs={{0,2},{1,3},{2,0},{3,1},{4,6},{5,7},{6,4},{7,5},{8,10},{9,11},{10,... | collective-permute-start | bytes 24584 | tf_op jit(solution)/shard_map/ppermute | solution.py:320
